TPU v7x, 256 devices: a whole 4x4x8 slice. The times are simulated.
256 devices in a mesh: tmpl: 32 (over x, y, core), grid: 8 (over z).
Axes of the slice: x: 4, y: 4, z: 8, core: 2. Of those that a mesh axis runs over, the one named last changes fastest.
Arguments:
- spectrum: float32 [1024, 64, 64, 128], P('tmpl', 'grid'), may hold values from -12 to 12
Outputs:
- best_scores: float32 [4, 64, 64, 64], P(None, 'grid', 'tmpl')
- coherence: float32 [64, 64, 64], P('grid', 'tmpl')
All inputs are finite; a program needn't handle non-finite values.
Results may differ from a plain program's by a relative error of at most 0.0001.
Values sent between devices are 32-bit elements; how exact they have to be, the bound alone decides.
No kernel may reach another device: no remote copies, remote signals or barrier semaphores. Data moves between devices by JAX's collectives and lax.ppermute only.
A program may use at most 128 MiB of HBM per device.

v0:
```python
import math

import jax
import jax.numpy as jnp
from jax import lax
from jax.sharding import Mesh
from jax.sharding import PartitionSpec as P

TOP = 4
TMPL = ("tmpl_0", "tmpl_1", "tmpl_2")


FLOOR = -1e30
SPREAD_FLOOR = 0.25


def copy_for_each(value, axis):
    copies = jnp.broadcast_to(value, (lax.axis_size(axis), *value.shape))
    return lax.all_to_all(copies, axis, split_axis=0, concat_axis=0, tiled=True)


def of_everyone(value, axis):
    everything = copy_for_each(value, axis)
    return jnp.sum(everything, axis=0)


def together(arrays, axis):
    ends = [0]
    for a in arrays:
        ends.append(ends[-1] + a.size)
    running = of_everyone(jnp.concatenate([a.ravel() for a in arrays]), axis)
    return tuple((running[b:e].reshape(a.shape) for a, b, e in zip(arrays, ends, ends[1:])))


def cut_along(value, dim, size):
    dims = value.shape
    tiles = value.reshape(*dims[:dim], size, dims[dim] // size, *dims[dim + 1 :])
    return jnp.moveaxis(tiles, dim, 0)


def laid_out(tiles, dim):
    dims = list(tiles.shape[1:])
    dims[dim] *= tiles.shape[0]
    return jnp.moveaxis(tiles, 0, dim).reshape(dims)


def exchange_in_order(tiles, axes, order):
    dims = [lax.axis_size(a) for a in axes]
    tiles = tiles.reshape(*dims, *tiles.shape[1:])
    for k in order:
        tiles = lax.all_to_all(tiles, axes[k], split_axis=k, concat_axis=k, tiled=True)
    return tiles.reshape(-1, *tiles.shape[len(axes) :])


def exchange_by_chip(value, groups, order, split_dim, concat_dim):
    size = lax.axis_size(groups[0]) * lax.axis_size(groups[1])
    tiles = cut_along(value, split_dim, size)
    return laid_out(exchange_in_order(tiles, groups, order), concat_dim)


def phase_table(length):
    order = jnp.arange(length, dtype=jnp.int32)
    turns = order[:, None] * order[None, :] % length
    angle = turns.astype(jnp.float32) * (2.0 * math.pi / length)
    return jnp.concatenate([jnp.cos(angle), -jnp.sin(angle)], axis=0)


def merge_top(former, latter):
    result = []
    for rank_out in range(len(former)):
        winner = jnp.maximum(former[rank_out], latter[rank_out])
        for rank_in in range(rank_out):
            winner = jnp.maximum(
                winner, jnp.minimum(former[rank_in], latter[rank_out - rank_in - 1])
            )
        result.append(winner)
    return tuple(result)


def fold_levels(leaders, running):
    while leaders[0].shape[0] > 1:
        number = leaders[0].shape[0]
        paired = tuple((value.reshape((number // 2, 2) + value.shape[1:]) for value in leaders))
        leaders = merge_top(
            tuple((value[:, 0] for value in paired)), tuple((value[:, 1] for value in paired))
        )
        folded = running.reshape((number // 2, 2) + running.shape[1:])
        running = folded[:, 0] + folded[:, 1]
    return (tuple((value[0] for value in leaders)), running[0])


def body(spectrum):
    local_tmpl, slab_rows, beta_rows, doubled = spectrum.shape
    points = doubled // 2
    paired_table = jnp.kron(jnp.eye(2, dtype=jnp.float32), phase_table(points))
    flat_rows = slab_rows * beta_rows // 2
    score = jnp.dot(
        spectrum.reshape(local_tmpl * flat_rows, 2 * doubled),
        paired_table,
        precision=lax.Precision.HIGHEST,
        preferred_element_type=jnp.float32,
    )
    score = score.reshape(local_tmpl, flat_rows, doubled)
    cell_count = float(points * points * points)
    sum_plain = jnp.sum(score, axis=(1, 2))
    sum_square = jnp.sum(score * score, axis=(1, 2))
    sum_plain, sum_square = together((sum_plain, sum_square), "grid")
    average = sum_plain / cell_count
    spread = sum_square / cell_count - average * average
    centred = score - average[:, None, None]
    normed = centred / jnp.sqrt(spread + SPREAD_FLOOR)[:, None, None]
    filler = jnp.full_like(normed, FLOOR)
    start = (normed,) + tuple((filler for rank_in in range(TOP - 1)))
    leaders, running = fold_levels(start, normed)
    line = beta_rows * points
    leaders = tuple((value.reshape(slab_rows, line) for value in leaders))
    running = running.reshape(slab_rows, line)
    groups = lax.axis_size(TMPL)
    piece = beta_rows // groups
    received = jax.tree.map(
        lambda part: exchange_by_chip(part, (("tmpl_0", "tmpl_1"), "tmpl_2"), (1, 0), 2, 0),
        tuple((value[None] for value in leaders)) + (running[None],),
    )
    best_parts, total_part = fold_levels(received[:-1], received[-1])
    best_scores = jnp.stack(best_parts, axis=0).reshape(TOP, slab_rows, piece, points)
    coherence = (total_part / math.sqrt(groups * local_tmpl)).reshape(slab_rows, piece, points)
    return (best_scores, coherence)


def solution(mesh):
    finer = Mesh(
        mesh.devices.reshape(4, 4, 2, mesh.shape["grid"]), ("tmpl_0", "tmpl_1", "tmpl_2", "grid")
    )
    placed = (P(TMPL, "grid", None, None),)
    return jax.shard_map(
        body,
        mesh=finer,
        in_specs=placed,
        out_specs=(P(None, "grid", TMPL, None), P("grid", TMPL, None)),
        check_vma=False,
    )
```

profile of v0, /device:TPU:2, one launch (start us, length us, event | category | flops | bytes accessed | tf_op | source)
XLA Modules:
  0.0 140.3 jit_solution(16316048197415630682)
XLA Ops:
  0.8 9.8 %reshape.1342 = f32[8192,256]{1,0:T(8,128)} reshape(f32[32,8,64,128]{3,2,1,0:T(8,128)} %param.1) | data formatting | bytes 16777216 | tf_op jit(solution)/shard_map/reshape | solution.py:98
  10.8 13.9 %multiply_reduce_fusion = (f32[8192]{0:T(1024)S(1)}, f32[128,8192]{1,0:T(8,128)}) fusion(f32[8192,256]{1,0:T(8,128)} %reshape.1342, f32[16,8,2,128]{3,2,1,0:T(2,128)S(1)} %bitcast.299), kind=kOutput, calls=%fused_computation.1 | convolution fusion | flops 3223314432 | bytes 12746752 | tf_op jit(solution)/shard_map/dot_general | solution.py:97
  24.8 2.4 %reduce_sum.31 = f32[8192]{0:T(1024)S(1)} reduce(f32[128,8192]{1,0:T(8,128)} %get-tuple-element.37, f32[]{:T(128)} %constant.25.clone.1), dimensions={0}, to_apply=%region_0.1 | reduce | flops 1040384 | bytes 4227076 | tf_op jit(solution)/shard_map/reduce_sum | solution.py:105
  28.1 8.5 %all-to-all-start = ((f32[8,1,64]{2,1,0:T(1,128)}), f32[8,1,64]{2,1,0:T(1,128)S(1)}, u32[]{:S(2)}, u32[]{:S(2)}) async-start(f32[8,1,64]{2,1,0:T(1,128)} %broadcast_in_dim.6), calls=%async_computation | async-start | bytes 8192 | tf_op jit(solution)/shard_map/all_to_all | solution.py:19
  36.5 6.6 %reshape.1343 = f32[16,2,256,128]{2,1,0,3:T(2,128)} reshape(f32[8192,128]{0,1:T(8,128)} %bitcast.276) | data formatting | bytes 8388608 | tf_op jit(solution)/shard_map/reshape | solution.py:103
  43.1 7.4 %copy.215 = f32[16,2,256,128]{3,2,0,1:T(8,128)} copy(f32[16,2,256,128]{2,1,0,3:T(2,128)} %reshape.1343) | data formatting | bytes 8388608 | tf_op jit(solution)/shard_map/reshape | solution.py:103
  50.9 2.8 %subtract_divide_fusion = f32[16,2,256,128]{3,2,0,1:T(8,128)S(1)} fusion(f32[16,2,256,128]{3,2,0,1:T(8,128)} %copy.215, f32[16,2]{0,1:T(2,128)S(1)} %copy.216, f32[16,2]{0,1:T(2,128)S(1)} %copy.214), kind=kLoop, calls=%fused_computation | loop fusion | flops 2097152 | bytes 8388864 | tf_op jit(solution)/shard_map/div | solution.py:111
  53.7 1.3 slice_add_fusion
  55.3 0.7 copy.258
  56.0 0.8 minimum_maximum_fusion.3
  57.7 0.7 copy.250
  58.4 3.4 %all-to-all-start.9 = ((f32[16,2,1,8,128]{4,3,0,2,1:T(8,128)}), f32[16,2,1,8,128]{4,3,0,2,1:T(8,128)S(1)}, u32[]{:S(2)}, u32[]{:S(2)}) async-start(f32[16,2,1,8,128]{4,3,0,2,1:T(8,128)} %copy.258), calls=%async_computation.9 | async-start | bytes 262144 | tf_op jit(solution)/shard_map/all_to_all | solution.py:51
  61.9 1.4 all-to-all-done.9
  63.2 3.4 %all-to-all-start.7 = ((f32[16,2,1,8,128]{4,3,0,2,1:T(8,128)}), f32[16,2,1,8,128]{4,3,0,2,1:T(8,128)S(1)}, u32[]{:S(2)}, u32[]{:S(2)}) async-start(f32[16,2,1,8,128]{4,3,0,2,1:T(8,128)} %copy.250), calls=%async_computation.7 | async-start | bytes 262144 | tf_op jit(solution)/shard_map/all_to_all | solution.py:51
  66.6 0.7 copy.259
  67.3 0.8 all-to-all-done.7
  68.1 3.8 %all_to_all.56 = f32[16,2,1,8,128]{4,3,0,2,1:T(8,128)S(1)} all-to-all(f32[16,2,1,8,128]{4,3,0,2,1:T(8,128)S(1)} %copy.239), channel_id=1, replica_groups=mesh['tmpl_0'=4,'tmpl_1'=4,'tmpl_2'=2,'grid'=8] {'tmpl_2'}, dimensions={1} | all-to-all | bytes 262144 | tf_op jit(solution)/shard_map/all_to_all | solution.py:51
  71.9 3.8 %all_to_all.57 = f32[16,2,1,8,128]{4,3,0,2,1:T(8,128)S(1)} all-to-all(f32[16,2,1,8,128]{4,3,0,2,1:T(8,128)S(1)} %copy.220), channel_id=1, replica_groups=mesh['tmpl_0'=4,'tmpl_1'=4,'tmpl_2'=2,'grid'=8] {'tmpl_2'}, dimensions={1} | all-to-all | bytes 262144 | tf_op jit(solution)/shard_map/all_to_all | solution.py:51
  75.7 3.8 %all_to_all.58 = f32[16,2,1,8,128]{4,3,0,2,1:T(8,128)S(1)} all-to-all(f32[16,2,1,8,128]{4,3,0,2,1:T(8,128)S(1)} %copy.229), channel_id=1, replica_groups=mesh['tmpl_0'=4,'tmpl_1'=4,'tmpl_2'=2,'grid'=8] {'tmpl_2'}, dimensions={1} | all-to-all | bytes 262144 | tf_op jit(solution)/shard_map/all_to_all | solution.py:51
  79.6 7.5 %all-to-all-start.10 = ((f32[16,2,1,8,128]{4,3,1,2,0:T(8,128)}), f32[16,2,1,8,128]{4,3,1,2,0:T(8,128)S(1)}, u32[]{:S(2)}, u32[]{:S(2)}) async-start(f32[16,2,1,8,128]{4,3,1,2,0:T(8,128)} %copy.259), calls=%async_computation.10 | async-start | bytes 262144 | tf_op jit(solution)/shard_map/all_to_all | solution.py:51
  87.0 0.7 copy.251
  87.7 0.7 copy.240
  89.7 3.8 %all-to-all-done.10 = f32[16,2,1,8,128]{4,3,1,2,0:T(8,128)S(1)} async-done(((f32[16,2,1,8,128]{4,3,1,2,0:T(8,128)}), f32[16,2,1,8,128]{4,3,1,2,0:T(8,128)S(1)}, u32[]{:S(2)}, u32[]{:S(2)}) %all-to-all-start.10) | async-done | bytes 131104 | tf_op jit(solution)/shard_map/all_to_all | solution.py:51
  93.4 5.1 %all-to-all-start.2 = ((f32[16,2,1,8,128]{4,3,1,2,0:T(8,128)}), f32[16,2,1,8,128]{4,3,1,2,0:T(8,128)S(1)}, u32[]{:S(2)}, u32[]{:S(2)}) async-start(f32[16,2,1,8,128]{4,3,1,2,0:T(8,128)} %copy.221), calls=%async_computation.2 | async-start | bytes 262144 | tf_op jit(solution)/shard_map/all_to_all | solution.py:51
  98.6 0.7 div.35
  99.2 5.6 %all-to-all-done.2 = f32[16,2,1,8,128]{4,3,1,2,0:T(8,128)S(1)} async-done(((f32[16,2,1,8,128]{4,3,1,2,0:T(8,128)}), f32[16,2,1,8,128]{4,3,1,2,0:T(8,128)S(1)}, u32[]{:S(2)}, u32[]{:S(2)}) %all-to-all-start.2) | async-done | bytes 131104 | tf_op jit(solution)/shard_map/all_to_all | solution.py:51
  104.9 5.1 %all-to-all-start.8 = ((f32[16,2,1,8,128]{4,3,1,2,0:T(8,128)}), f32[16,2,1,8,128]{4,3,1,2,0:T(8,128)S(1)}, u32[]{:S(2)}, u32[]{:S(2)}) async-start(f32[16,2,1,8,128]{4,3,1,2,0:T(8,128)} %copy.251), calls=%async_computation.8 | async-start | bytes 262144 | tf_op jit(solution)/shard_map/all_to_all | solution.py:51
  110.0 6.4 %all-to-all-done.8 = f32[16,2,1,8,128]{4,3,1,2,0:T(8,128)S(1)} async-done(((f32[16,2,1,8,128]{4,3,1,2,0:T(8,128)}), f32[16,2,1,8,128]{4,3,1,2,0:T(8,128)S(1)}, u32[]{:S(2)}, u32[]{:S(2)}) %all-to-all-start.8) | async-done | bytes 131104 | tf_op jit(solution)/shard_map/all_to_all | solution.py:51
  116.3 5.1 %all-to-all-start.6 = ((f32[16,2,1,8,128]{4,3,1,2,0:T(8,128)}), f32[16,2,1,8,128]{4,3,1,2,0:T(8,128)S(1)}, u32[]{:S(2)}, u32[]{:S(2)}) async-start(f32[16,2,1,8,128]{4,3,1,2,0:T(8,128)} %copy.240), calls=%async_computation.6 | async-start | bytes 262144 | tf_op jit(solution)/shard_map/all_to_all | solution.py:51
  121.4 6.4 %all-to-all-done.6 = f32[16,2,1,8,128]{4,3,1,2,0:T(8,128)S(1)} async-done(((f32[16,2,1,8,128]{4,3,1,2,0:T(8,128)}), f32[16,2,1,8,128]{4,3,1,2,0:T(8,128)S(1)}, u32[]{:S(2)}, u32[]{:S(2)}) %all-to-all-start.6) | async-done | bytes 131104 | tf_op jit(solution)/shard_map/all_to_all | solution.py:51
  127.8 5.1 %all-to-all-start.4 = ((f32[16,2,1,8,128]{4,3,1,2,0:T(8,128)}), f32[16,2,1,8,128]{4,3,1,2,0:T(8,128)S(1)}, u32[]{:S(2)}, u32[]{:S(2)}) async-start(f32[16,2,1,8,128]{4,3,1,2,0:T(8,128)} %copy.230), calls=%async_computation.4 | async-start | bytes 262144 | tf_op jit(solution)/shard_map/all_to_all | solution.py:51
  132.8 6.4 %all-to-all-done.4 = f32[16,2,1,8,128]{4,3,1,2,0:T(8,128)S(1)} async-done(((f32[16,2,1,8,128]{4,3,1,2,0:T(8,128)}), f32[16,2,1,8,128]{4,3,1,2,0:T(8,128)S(1)}, u32[]{:S(2)}, u32[]{:S(2)}) %all-to-all-start.4) | async-done | bytes 131104 | tf_op jit(solution)/shard_map/all_to_all | solution.py:51
  (58 shorter events, 5.2 us)
Async XLA Ops:
  28.1 22.4 %all-to-all-start = ((f32[8,1,64]{2,1,0:T(1,128)}), f32[8,1,64]{2,1,0:T(1,128)S(1)}, u32[]{:S(2)}, u32[]{:S(2)}) async-start(f32[8,1,64]{2,1,0:T(1,128)} %broadcast_in_dim.6), calls=%async_computation | async-start | bytes 8192 | tf_op jit(solution)/shard_map/all_to_all | solution.py:19
  58.4 4.8 %all-to-all-start.9 = ((f32[16,2,1,8,128]{4,3,0,2,1:T(8,128)}), f32[16,2,1,8,128]{4,3,0,2,1:T(8,128)S(1)}, u32[]{:S(2)}, u32[]{:S(2)}) async-start(f32[16,2,1,8,128]{4,3,0,2,1:T(8,128)} %copy.258), calls=%async_computation.9 | async-start | bytes 262144 | tf_op jit(solution)/shard_map/all_to_all | solution.py:51
  63.2 4.8 %all-to-all-start.7 = ((f32[16,2,1,8,128]{4,3,0,2,1:T(8,128)}), f32[16,2,1,8,128]{4,3,0,2,1:T(8,128)S(1)}, u32[]{:S(2)}, u32[]{:S(2)}) async-start(f32[16,2,1,8,128]{4,3,0,2,1:T(8,128)} %copy.250), calls=%async_computation.7 | async-start | bytes 262144 | tf_op jit(solution)/shard_map/all_to_all | solution.py:51
  79.6 13.9 %all-to-all-start.10 = ((f32[16,2,1,8,128]{4,3,1,2,0:T(8,128)}), f32[16,2,1,8,128]{4,3,1,2,0:T(8,128)S(1)}, u32[]{:S(2)}, u32[]{:S(2)}) async-start(f32[16,2,1,8,128]{4,3,1,2,0:T(8,128)} %copy.259), calls=%async_computation.10 | async-start | bytes 262144 | tf_op jit(solution)/shard_map/all_to_all | solution.py:51
  93.4 11.4 %all-to-all-start.2 = ((f32[16,2,1,8,128]{4,3,1,2,0:T(8,128)}), f32[16,2,1,8,128]{4,3,1,2,0:T(8,128)S(1)}, u32[]{:S(2)}, u32[]{:S(2)}) async-start(f32[16,2,1,8,128]{4,3,1,2,0:T(8,128)} %copy.221), calls=%async_computation.2 | async-start | bytes 262144 | tf_op jit(solution)/shard_map/all_to_all | solution.py:51
  104.9 11.4 %all-to-all-start.8 = ((f32[16,2,1,8,128]{4,3,1,2,0:T(8,128)}), f32[16,2,1,8,128]{4,3,1,2,0:T(8,128)S(1)}, u32[]{:S(2)}, u32[]{:S(2)}) async-start(f32[16,2,1,8,128]{4,3,1,2,0:T(8,128)} %copy.251), calls=%async_computation.8 | async-start | bytes 262144 | tf_op jit(solution)/shard_map/all_to_all | solution.py:51
  116.3 11.4 %all-to-all-start.6 = ((f32[16,2,1,8,128]{4,3,1,2,0:T(8,128)}), f32[16,2,1,8,128]{4,3,1,2,0:T(8,128)S(1)}, u32[]{:S(2)}, u32[]{:S(2)}) async-start(f32[16,2,1,8,128]{4,3,1,2,0:T(8,128)} %copy.240), calls=%async_computation.6 | async-start | bytes 262144 | tf_op jit(solution)/shard_map/all_to_all | solution.py:51
  127.8 11.4 %all-to-all-start.4 = ((f32[16,2,1,8,128]{4,3,1,2,0:T(8,128)}), f32[16,2,1,8,128]{4,3,1,2,0:T(8,128)S(1)}, u32[]{:S(2)}, u32[]{:S(2)}) async-start(f32[16,2,1,8,128]{4,3,1,2,0:T(8,128)} %copy.230), calls=%async_computation.4 | async-start | bytes 262144 | tf_op jit(solution)/shard_map/all_to_all | solution.py:51
where the time goes:
time: 143 us; the launch traced here: 140 us
  starting transfers between devices  42.9 us (30%)
  local copies, waits for them, and re-layouts  30.7 us (21%)
  waiting for transfers between devices  30.6 us (21%)
  matrix products  13.9 us (10%)
  blocking collectives  11.5 us (8%)
  other arithmetic  9.76 us (7%)
    all_to_all x7, starting transfers between devices, exchange_in_order(): lax.all_to_all(tiles, axes[k], split_axis=k, concat_axis=k, tiled=True)  34.4 us
    all_to_all x7, waiting for transfers between devices, exchange_in_order(): lax.all_to_all(tiles, axes[k], split_axis=k, concat_axis=k, tiled=True)  30.6 us
    reshape x2, local copies, waits for them, and re-layouts, body(): score = score.reshape(local_tmpl, flat_rows, doubled)  13.9 us
    dot_general x1, matrix products, body(): jnp.dot(spectrum.reshape(local_tmpl * flat_rows, 2 * doubled), paired_tab...  13.9 us
    all_to_all x3, blocking collectives, exchange_in_order(): lax.all_to_all(tiles, axes[k], split_axis=k, concat_axis=k, tiled=True)  11.5 us
    reshape x1, local copies, waits for them, and re-layouts, body(): spectrum.reshape(local_tmpl * flat_rows, 2 * doubled)  9.84 us
    all_to_all x1, starting transfers between devices, copy_for_each(): return lax.all_to_all(copies, axis, split_axis=0, concat_axis=0, tiled=True)  8.46 us
    all_to_all x10, local copies, waits for them, and re-layouts, exchange_in_order(): lax.all_to_all(tiles, axes[k], split_axis=k, concat_axis=k, tiled=True)  3.33 us
  transfers between devices with their start and end apart: 8, of which 7 were waited for; matrix products, arithmetic and copies ran while one was open for 13% of the time, Pallas kernels for 0%

commit v1 on v0

v1 whole, which is shorter than its diff:
```python
import functools
import math

import jax
import jax.numpy as jnp
import numpy as np
from jax import lax
from jax.experimental import pallas as pl
from jax.experimental.pallas import tpu as pltpu
from jax.sharding import Mesh
from jax.sharding import PartitionSpec as P

TOP = 4
SPREAD_FLOOR = 0.25
ROWS = 8
LANES = 128
XY = ("tmpl_0", "tmpl_1")
CORE = "tmpl_2"


def split_table(points):
    order = np.arange(points)
    angle = (order[:, None] * order[None, :] % points) * (2.0 * math.pi / points)
    table = np.concatenate([np.cos(angle), -np.sin(angle)], axis=0)
    mirror = (points - order) % points
    table[:points] = 0.5 * (table[:points] + table[:points][mirror])
    table[points:] = 0.5 * (table[points:] - table[points:][mirror])
    high = table.astype(jnp.bfloat16)
    low = (table - high.astype(np.float64)).astype(jnp.bfloat16)
    pair = [np.kron(np.eye(2), part.astype(np.float64)) for part in (high, low)]
    return np.concatenate(pair, axis=1).astype(jnp.bfloat16)


def to_row(column):
    count = column.shape[0]
    sub = lax.broadcasted_iota(jnp.int32, (count, LANES), 0)
    lane = lax.broadcasted_iota(jnp.int32, (count, LANES), 1)
    return jnp.sum(jnp.where(sub == lane, column, 0.0), axis=0, keepdims=True)


def to_column(row, count):
    sub = lax.broadcasted_iota(jnp.int32, (count, LANES), 0)
    lane = lax.broadcasted_iota(jnp.int32, (count, LANES), 1)
    kept = jnp.sum(jnp.where(sub == lane, row, 0.0), axis=1, keepdims=True)
    return jnp.broadcast_to(kept, (count, LANES))


def score_kernel(x_hbm, w_ref, mine_ref, send_ref, stat_ref, x_vmem, plain, square, sems):
    tmpls, slab, beta, doubled = x_vmem.shape
    pairs = beta // 4
    core = lax.axis_index(CORE)

    def fetch(t):
        return pltpu.make_async_copy(x_hbm.at[t], x_vmem.at[t], sems.at[t])

    for t in range(tmpls):
        fetch(t).start()

    def advance(t, carry):
        fetch(t).wait()
        plain_t = square_t = None
        for parity, out in ((core, mine_ref), (1 - core, send_ref)):
            sides = [
                x_vmem[t, :, pl.ds(2 * parity + h, pairs, stride=4), :].reshape(slab * pairs, doubled)
                for h in range(2)
            ]
            x = jnp.concatenate(sides, axis=1)
            high = x.astype(jnp.bfloat16)
            rest = x - high.astype(jnp.float32)
            mid = rest.astype(jnp.bfloat16)
            low = (rest - mid.astype(jnp.float32)).astype(jnp.bfloat16)
            w = w_ref[...]
            dot = functools.partial(jnp.dot, preferred_element_type=jnp.float32)
            both = dot(low, w) + dot(mid, w) + dot(high, w)
            s = both[:, :LANES] + both[:, LANES:]
            out[t] = s.reshape(slab, pairs, LANES)
            p = jnp.sum(s.reshape(-1, ROWS, LANES), axis=0)
            q = jnp.sum((s * s).reshape(-1, ROWS, LANES), axis=0)
            plain_t = p if plain_t is None else plain_t + p
            square_t = q if square_t is None else square_t + q
        plain[t] = plain_t
        square[t] = square_t
        return carry

    lax.fori_loop(0, tmpls, advance, 0)
    rows = []
    for part in (plain, square):
        whole = jnp.sum(part[...], axis=1)
        rows.append(to_row(jnp.sum(whole, axis=1, keepdims=True)))
    sub = lax.broadcasted_iota(jnp.int32, (ROWS, LANES), 0)
    tile = jnp.where(sub == 0, rows[0], jnp.where(sub == 1, rows[1], 0.0))
    stat_ref[...] = jnp.broadcast_to(tile[None], stat_ref.shape)


def order(a, b):
    return jnp.maximum(a, b), jnp.minimum(a, b)


def sort4(a, b, c, d):
    a, b = order(a, b)
    c, d = order(c, d)
    a, c = order(a, c)
    b, d = order(b, d)
    b, c = order(b, c)
    return a, b, c, d


def merge4(u, v):
    a, b, c, d = (jnp.maximum(u[i], v[3 - i]) for i in range(4))
    a, c = order(a, c)
    b, d = order(b, d)
    a, b = order(a, b)
    c, d = order(c, d)
    return a, b, c, d


def top_kernel(count, mine_ref, other_ref, stat_ref, out_ref, gain_ref, shift_ref):
    tmpls, slab, pairs, _ = mine_ref.shape
    peers = stat_ref.shape[0] // 2
    for half in range(2):
        total = jnp.sum(stat_ref[half * peers : (half + 1) * peers], axis=0)
        average = total[0:1] / count
        spread = total[1:2] / count - average * average
        gain = 1.0 / jnp.sqrt(spread + SPREAD_FLOOR)
        gain_ref[pl.ds(half * tmpls, tmpls)] = to_column(gain, tmpls)
        shift_ref[pl.ds(half * tmpls, tmpls)] = to_column(average, tmpls)
    core = lax.axis_index(CORE)
    firsts = (core * tmpls, (1 - core) * tmpls)

    def tile(a, carry):
        for q in range(pairs // ROWS):
            best = total = None
            for first, ref in zip(firsts, (mine_ref, other_ref)):
                for group in range(tmpls // 4):
                    four = []
                    for t in range(4 * group, 4 * group + 4):
                        s = ref[t, a, pl.ds(q * ROWS, ROWS)]
                        g = gain_ref[pl.ds(first + t, ROWS, stride=0)]
                        m = shift_ref[pl.ds(first + t, ROWS, stride=0)]
                        four.append((s - m) * g)
                    part = (four[0] + four[1]) + (four[2] + four[3])
                    total = part if total is None else total + part
                    four = sort4(*four)
                    best = four if best is None else merge4(best, four)
            for r, value in enumerate((*best, total)):
                start = (q * ROWS * (TOP + 1) + r) * slab + a
                out_ref[pl.ds(start, ROWS, stride=(TOP + 1) * slab)] = value
        return carry

    lax.fori_loop(0, slab, tile, 0)


def final_kernel(norm, in_ref, best_ref, sum_ref):
    peers = in_ref.shape[0]
    points = best_ref.shape[-1]
    fours = [tuple(in_ref[p, r] for r in range(TOP)) for p in range(peers)]
    total = in_ref[0, TOP]
    for p in range(1, peers):
        total = total + in_ref[p, TOP]
    while len(fours) > 1:
        fours = [merge4(u, v) for u, v in zip(fours[::2], fours[1::2])]
    total = total / norm
    for h in range(2):
        lanes = slice(h * points, (h + 1) * points)
        for r in range(TOP):
            best_ref[r, :, h, :] = fours[0][r][:, lanes]
        sum_ref[:, h, :] = total[:, lanes]


def body(spectrum):
    tmpls, slab, beta, doubled = spectrum.shape
    points = doubled // 2
    pairs = beta // 4
    chips = lax.axis_size(XY)
    peers = 2 * lax.axis_size("grid")
    vmem = pl.BlockSpec(memory_space=pltpu.VMEM)
    part = jax.ShapeDtypeStruct((tmpls, slab, pairs, LANES), jnp.float32)
    mine, send, stat = pl.pallas_call(
        score_kernel,
        out_shape=(part, part, jax.ShapeDtypeStruct((peers, ROWS, LANES), jnp.float32)),
        in_specs=[pl.BlockSpec(memory_space=pl.ANY), vmem],
        out_specs=(vmem, vmem, vmem),
        scratch_shapes=[
            pltpu.VMEM(spectrum.shape, jnp.float32),
            pltpu.VMEM((tmpls, ROWS, LANES), jnp.float32),
            pltpu.VMEM((tmpls, ROWS, LANES), jnp.float32),
            pltpu.SemaphoreType.DMA((tmpls,)),
        ],
        compiler_params=pltpu.CompilerParams(vmem_limit_bytes=40 * 2**20),
        name="scores",
    )(spectrum, jnp.asarray(split_table(points)))
    stats = lax.all_to_all(stat, (CORE, "grid"), split_axis=0, concat_axis=0, tiled=True)
    other = lax.ppermute(send, CORE, [(0, 1), (1, 0)])
    packed = pl.pallas_call(
        functools.partial(top_kernel, float(points**3)),
        out_shape=jax.ShapeDtypeStruct((chips * (TOP + 1) * slab, LANES), jnp.float32),
        in_specs=[vmem, vmem, vmem],
        out_specs=vmem,
        scratch_shapes=[
            pltpu.VMEM((2 * tmpls, LANES), jnp.float32),
            pltpu.VMEM((2 * tmpls, LANES), jnp.float32),
        ],
        compiler_params=pltpu.CompilerParams(vmem_limit_bytes=20 * 2**20),
        name="tops",
    )(mine, other, stats)
    packed = packed.reshape(chips, TOP + 1, slab, LANES)
    received = lax.all_to_all(packed, XY, split_axis=0, concat_axis=0, tiled=True)
    return pl.pallas_call(
        functools.partial(final_kernel, math.sqrt(2 * chips * tmpls)),
        out_shape=(
            jax.ShapeDtypeStruct((TOP, slab, 2, points), jnp.float32),
            jax.ShapeDtypeStruct((slab, 2, points), jnp.float32),
        ),
        in_specs=[vmem],
        out_specs=(vmem, vmem),
        name="finish",
    )(received)


def solution(mesh):
    finer = Mesh(
        mesh.devices.reshape(4, 4, 2, mesh.shape["grid"]), (*XY, CORE, "grid")
    )
    tmpl = (*XY, CORE)
    return jax.shard_map(
        body,
        mesh=finer,
        in_specs=(P(tmpl, "grid", None, None),),
        out_specs=(P(None, "grid", tmpl, None), P("grid", tmpl, None)),
        check_vma=False,
    )
```

time: 143 us -> 50 us (0.35); the launches traced: 140 us -> 49.2 us
  starting transfers between devices: 42.9 us -> 0.09 us
  waiting for transfers between devices: 30.6 us -> 0.01 us
  local copies, waits for them, and re-layouts: 30.7 us -> 4.28 us
  blocking collectives: 11.5 us -> 31 us
  matrix products: 13.9 us -> 0 us
  Pallas kernels: 0 us -> 13.2 us
  other arithmetic: 9.76 us -> 0 us
    all_to_all x8 -> x0, starting transfers between devices: 42.9 us -> none  [the longest x7 34.4 us: exchange_in_order(): lax.all_to_all(tiles, axes[k], split_axis=k, concat_axis=k, tiled=True)]
    all_to_all x8 -> x0, waiting for transfers between devices: 30.6 us -> none  [the longest x7 30.6 us: exchange_in_order(): lax.all_to_all(tiles, axes[k], split_axis=k, concat_axis=k, tiled=True)]
    reshape x8 -> x0, local copies, waits for them, and re-layouts: 25.5 us -> none  [the longest x2 13.9 us: body(): score = score.reshape(local_tmpl, flat_rows, doubled)]
    all_to_all x3 -> x2, blocking collectives: 11.5 us -> 31 us  [the longest x1 16.4 us: body(): lax.all_to_all(stat, (CORE, 'grid'), split_axis=0, concat_axis=0, tiled=T...]
    dot_general x1 -> x0, matrix products: 13.9 us -> none  [body(): jnp.dot(spectrum.reshape(local_tmpl * flat_rows, 2 * doubled), paired_tab...]
    pallas_call x0 -> x3, Pallas kernels: none -> 13.2 us  [the longest x1 10 us: body(): pl.pallas_call(score_kernel, out_shape=(part, part, jax.ShapeDtypeStruct(...]
    unnamed x0 -> x4, local copies, waits for them, and re-layouts: none -> 4.28 us
    all_to_all x10 -> x0, local copies, waits for them, and re-layouts: 3.33 us -> none  [exchange_in_order(): lax.all_to_all(tiles, axes[k], split_axis=k, concat_axis=k, tiled=True)]
  transfers between devices with their start and end apart: 8 -> 1, of which waited for: 7 -> 0; matrix products, arithmetic and copies ran while one was open for 13% -> 0% of each run, Pallas kernels for 0% -> 0%
where the time goes in v1:
time: 50 us; the launch traced here: 49.2 us
  blocking collectives  31 us (62%)
  Pallas kernels  13.2 us (26%)
  local copies, waits for them, and re-layouts  4.28 us (9%)
  between operations  0.66 us (1%)
    all_to_all x1, blocking collectives, body(): lax.all_to_all(stat, (CORE, 'grid'), split_axis=0, concat_axis=0, tiled=T...  16.4 us
    all_to_all x1, blocking collectives, body(): lax.all_to_all(packed, XY, split_axis=0, concat_axis=0, tiled=True)  14.6 us
    pallas_call x1, Pallas kernels, body(): pl.pallas_call(score_kernel, out_shape=(part, part, jax.ShapeDtypeStruct(...  10 us
    unnamed x4, local copies, waits for them, and re-layouts  4.28 us
    pallas_call x1, Pallas kernels, body(): pl.pallas_call(functools.partial(final_kernel, math.sqrt(2 * chips * tmpl...  1.72 us
    pallas_call x1, Pallas kernels, body(): pl.pallas_call(functools.partial(top_kernel, float(points ** 3)), out_sha...  1.42 us
  transfers between devices with their start and end apart: 1, of which 0 were waited for; matrix products, arithmetic and copies ran while one was open for 0% of the time, Pallas kernels for 0%

profile of v1, /device:TPU:2, one launch (start us, length us, event | category | flops | bytes accessed | tf_op | source)
XLA Modules:
  0.0 49.2 jit_solution(7028599467998331008)
XLA Ops:
  0.6 0.0 copy-start
  0.6 3.4 %copy-done = f32[32,8,64,128]{3,2,1,0:T(8,128)S(1)} copy-done((f32[32,8,64,128]{3,2,1,0:T(8,128)S(1)}, f32[32,8,64,128]{3,2,1,0:T(8,128)}, u32[]{:S(2)}) %copy-start) | copy-done | bytes 8388632
  4.0 0.0 copy-start.1
  4.0 0.9 %copy-done.1 = bf16[256,256]{1,0:T(8,128)(2,1)S(1)} copy-done((bf16[256,256]{1,0:T(8,128)(2,1)S(1)}, bf16[256,256]{1,0:T(8,128)(2,1)}, u32[]{:S(2)}) %copy-start.1) | copy-done | bytes 131096
  4.9 10.0 %scores.1 = (f32[32,8,16,128]{3,2,1,0:T(8,128)S(1)}, f32[32,8,16,128]{3,2,1,0:T(8,128)S(1)}, f32[16,8,128]{2,1,0:T(8,128)S(1)}) custom-call(f32[32,8,64,128]{3,2,1,0:T(8,128)S(1)} %copy-done, bf16[256,256]{1,0:T(8,128)(2,1)S(1)} %copy-done.1), custom_call_target="tpu_custom_call" | custom-call | tf_op jit(solution)/shard_map/scores/pallas_call | solution.py:178
  15.0 0.1 collective-permute-start
  15.1 16.4 %all_to_all.10.stat_ref = f32[16,8,128]{2,1,0:T(8,128)S(1)} all-to-all(f32[16,8,128]{2,1,0:T(8,128)S(1)} %get-tuple-element.7), channel_id=1, replica_groups=mesh['tmpl_0'=4,'tmpl_1'=4,'tmpl_2'=2,'grid'=8] {'tmpl_2','grid'}, dimensions={0} | all-to-all | bytes 131072 | tf_op jit(solution)/shard_map/all_to_all | solution.py:192
  31.5 0.0 collective-permute-done.other_ref
  31.5 1.4 %tops.1 = f32[640,128]{1,0:T(8,128)S(1)} custom-call(f32[32,8,16,128]{3,2,1,0:T(8,128)S(1)} %get-tuple-element.5.mine_ref, f32[32,8,16,128]{3,2,1,0:T(8,128)S(1)} %collective-permute-done.other_ref, f32[16,8,128]{2,1,0:T(8,128)S(1)} %all_to_all.10.stat_ref), custom_call_target="tpu_custom_call" | custom-call | tf_op jit(solution)/shard_map/tops/pallas_call | solution.py:194
  32.9 14.6 %all_to_all.11.in_ref = f32[16,5,8,128]{3,2,1,0:T(8,128)} all-to-all(f32[16,5,8,128]{3,2,1,0:T(8,128)S(1)} %bitcast.1), channel_id=1, replica_groups=mesh['tmpl_0'=4,'tmpl_1'=4,'tmpl_2'=2,'grid'=8] {'tmpl_0','tmpl_1'}, dimensions={0} | all-to-all | bytes 655360 | tf_op jit(solution)/shard_map/all_to_all | solution.py:207
  47.5 1.7 %finish.1 = (f32[4,8,2,64]{3,2,1,0:T(2,128)}, f32[8,2,64]{2,1,0:T(2,128)}) custom-call(f32[16,5,8,128]{3,2,1,0:T(8,128)} %all_to_all.11.in_ref), custom_call_target="tpu_custom_call" | custom-call | tf_op jit(solution)/shard_map/finish/pallas_call | solution.py:208
Async XLA Ops:
  0.6 3.4 %copy-start = (f32[32,8,64,128]{3,2,1,0:T(8,128)S(1)}, f32[32,8,64,128]{3,2,1,0:T(8,128)}, u32[]{:S(2)}) copy-start(f32[32,8,64,128]{3,2,1,0:T(8,128)} %x_hbm.1) | copy-start | bytes 25165828
  4.0 0.9 %copy-start.1 = (bf16[256,256]{1,0:T(8,128)(2,1)S(1)}, bf16[256,256]{1,0:T(8,128)(2,1)}, u32[]{:S(2)}) copy-start(bf16[256,256]{1,0:T(8,128)(2,1)} %constant.2.clone.w_ref) | copy-start | bytes 393220
  15.0 16.5 %collective-permute-start = (f32[32,8,16,128]{3,2,1,0:T(8,128)S(1)}, f32[32,8,16,128]{3,2,1,0:T(8,128)S(1)}, u32[]{:S(2)}, u32[]{:S(2)}) collective-permute-start(f32[32,8,16,128]{3,2,1,0:T(8,128)S(1)} %get-tuple-element.6), channel_id=1, source_target_pairs={{0,8},{8,0},{1,9},{9,1},{2,10},{10,2},{3,11},{11,3},{4,12},{12,4},... | collective-permute-start | bytes 6291464 | tf_op jit(solution)/shard_map/ppermute | solution.py:193

commit v2 on v1

--- a/solution.py
+++ b/solution.py
@@ -14,6 +14,7 @@
 SPREAD_FLOOR = 0.25
 ROWS = 8
 LANES = 128
+GROUP = 4
 XY = ("tmpl_0", "tmpl_1")
 CORE = "tmpl_2"
 
@@ -45,50 +46,83 @@
     return jnp.broadcast_to(kept, (count, LANES))
 
 
-def score_kernel(x_hbm, w_ref, mine_ref, send_ref, stat_ref, x_vmem, plain, square, sems):
+def score_kernel(
+    x_hbm, w_hbm, mine_ref, send_ref, stat_ref, x_vmem, w_vmem, plain, square, sems, w_sem
+):
     tmpls, slab, beta, doubled = x_vmem.shape
     pairs = beta // 4
+    rows = slab * pairs
     core = lax.axis_index(CORE)
-
-    def fetch(t):
-        return pltpu.make_async_copy(x_hbm.at[t], x_vmem.at[t], sems.at[t])
-
-    for t in range(tmpls):
-        fetch(t).start()
-
-    def advance(t, carry):
-        fetch(t).wait()
-        plain_t = square_t = None
-        for parity, out in ((core, mine_ref), (1 - core, send_ref)):
-            sides = [
-                x_vmem[t, :, pl.ds(2 * parity + h, pairs, stride=4), :].reshape(slab * pairs, doubled)
-                for h in range(2)
-            ]
-            x = jnp.concatenate(sides, axis=1)
-            high = x.astype(jnp.bfloat16)
-            rest = x - high.astype(jnp.float32)
-            mid = rest.astype(jnp.bfloat16)
-            low = (rest - mid.astype(jnp.float32)).astype(jnp.bfloat16)
-            w = w_ref[...]
-            dot = functools.partial(jnp.dot, preferred_element_type=jnp.float32)
-            both = dot(low, w) + dot(mid, w) + dot(high, w)
-            s = both[:, :LANES] + both[:, LANES:]
-            out[t] = s.reshape(slab, pairs, LANES)
-            p = jnp.sum(s.reshape(-1, ROWS, LANES), axis=0)
-            q = jnp.sum((s * s).reshape(-1, ROWS, LANES), axis=0)
-            plain_t = p if plain_t is None else plain_t + p
-            square_t = q if square_t is None else square_t + q
-        plain[t] = plain_t
-        square[t] = square_t
-        return carry
-
-    lax.fori_loop(0, tmpls, advance, 0)
-    rows = []
+    parities = (core, 1 - core)
+    outs = (mine_ref, send_ref)
+
+    def fetch(g):
+        block = pl.ds(g * GROUP, GROUP)
+        return pltpu.make_async_copy(x_hbm.at[block], x_vmem.at[block], sems.at[g])
+
+    table = pltpu.make_async_copy(w_hbm, w_vmem, w_sem)
+    table.start()
+    for g in range(tmpls // GROUP):
+        fetch(g).start()
+    table.wait()
+
+    def parts(t, parity):
+        sides = [
+            x_vmem[t, :, pl.ds(2 * parity + h, pairs, stride=4), :].reshape(rows, doubled)
+            for h in range(2)
+        ]
+        x = jnp.concatenate(sides, axis=1)
+        high = x.astype(jnp.bfloat16)
+        rest = x - high.astype(jnp.float32)
+        mid = rest.astype(jnp.bfloat16)
+        low = (rest - mid.astype(jnp.float32)).astype(jnp.bfloat16)
+        return low, mid, high
+
+    def run(*accs):
+        first, accs = accs[:2], accs[2:]
+        for m in range(2):
+            pltpu.matmul_push_rhs(w_vmem[...], staging_register=0, mxu_index=m)
+            zeros = jnp.zeros((16, 2 * doubled), jnp.bfloat16)
+            pltpu.matmul_acc_lhs(first[m], zeros, load_staged_rhs=0)
+            pltpu.matmul_pop(first[m])
+
+        def take(t, u):
+            plain_t = square_t = None
+            for m in range(2):
+                both = pltpu.matmul_pop(accs[2 * u + m])
+                s = both[:, :LANES] + both[:, LANES:]
+                outs[m][t] = s.reshape(slab, pairs, LANES)
+                p = jnp.sum(s.reshape(-1, ROWS, LANES), axis=0)
+                q = jnp.sum((s * s).reshape(-1, ROWS, LANES), axis=0)
+                plain_t = p if plain_t is None else plain_t + p
+                square_t = q if square_t is None else square_t + q
+            plain[t] = plain_t
+            square[t] = square_t
+
+        def advance(g, carry):
+            fetch(g).wait()
+            for u in range(GROUP):
+                for m in range(2):
+                    for part in parts(g * GROUP + u, parities[m]):
+                        pltpu.matmul_acc_lhs(accs[2 * (u % 4) + m], part)
+                if u:
+                    take(g * GROUP + u - 1, (u - 1) % 4)
+            take(g * GROUP + GROUP - 1, (GROUP - 1) % 4)
+            return carry
+
+        lax.fori_loop(0, tmpls // GROUP, advance, 0)
+
+    pl.run_scoped(
+        run,
+        *(pltpu.ACC(m)((16, 256), jnp.float32) for m in range(2)),
+        *(pltpu.ACC(m)((rows, 256), jnp.float32) for _ in range(4) for m in range(2)),
+    )
+    totals = []
     for part in (plain, square):
         whole = jnp.sum(part[...], axis=1)
-        rows.append(to_row(jnp.sum(whole, axis=1, keepdims=True)))
+        totals.append(to_row(jnp.sum(whole, axis=1, keepdims=True)))
     sub = lax.broadcasted_iota(jnp.int32, (ROWS, LANES), 0)
-    tile = jnp.where(sub == 0, rows[0], jnp.where(sub == 1, rows[1], 0.0))
+    tile = jnp.where(sub == 0, totals[0], jnp.where(sub == 1, totals[1], 0.0))
     stat_ref[...] = jnp.broadcast_to(tile[None], stat_ref.shape)
 
 
@@ -178,17 +212,22 @@
     mine, send, stat = pl.pallas_call(
         score_kernel,
         out_shape=(part, part, jax.ShapeDtypeStruct((peers, ROWS, LANES), jnp.float32)),
-        in_specs=[pl.BlockSpec(memory_space=pl.ANY), vmem],
+        in_specs=[pl.BlockSpec(memory_space=pltpu.HBM)] * 2,
         out_specs=(vmem, vmem, vmem),
         scratch_shapes=[
             pltpu.VMEM(spectrum.shape, jnp.float32),
+            pltpu.VMEM((2 * doubled, 2 * doubled), jnp.bfloat16),
             pltpu.VMEM((tmpls, ROWS, LANES), jnp.float32),
             pltpu.VMEM((tmpls, ROWS, LANES), jnp.float32),
-            pltpu.SemaphoreType.DMA((tmpls,)),
+            pltpu.SemaphoreType.DMA((tmpls // GROUP,)),
+            pltpu.SemaphoreType.DMA,
         ],
         compiler_params=pltpu.CompilerParams(vmem_limit_bytes=40 * 2**20),
         name="scores",
-    )(spectrum, jnp.asarray(split_table(points)))
+    )(*(
+        pltpu.with_memory_space_constraint(a, pltpu.HBM)
+        for a in (spectrum, jnp.asarray(split_table(points)))
+    ))
     stats = lax.all_to_all(stat, (CORE, "grid"), split_axis=0, concat_axis=0, tiled=True)
     other = lax.ppermute(send, CORE, [(0, 1), (1, 0)])
     packed = pl.pallas_call(
@@ -213,6 +252,7 @@
         ),
         in_specs=[vmem],
         out_specs=(vmem, vmem),
+        compiler_params=pltpu.CompilerParams(vmem_limit_bytes=8 * 2**20),
         name="finish",
     )(received)
 

time: 50 us -> 42.4 us (0.85)
  local copies, waits for them, and re-layouts: 4.28 us -> 0 us
  Pallas kernels: 13.2 us -> 10.1 us
    unnamed x4 -> x0, local copies, waits for them, and re-layouts: 4.28 us -> none
    pallas_call x1, Pallas kernels: 10 us -> 7.97 us  [body(): pl.pallas_call(score_kernel, out_shape=(part, part, jax.ShapeDtypeStruct(...]
    pallas_call x1, Pallas kernels: 1.72 us -> 0.75 us  [body(): pl.pallas_call(functools.partial(final_kernel, math.sqrt(2 * chips * tmpl...]
where the time goes in v2:
time: 42.4 us; the launch traced here: 41.8 us
  blocking collectives  30.9 us (73%)
  Pallas kernels  10.1 us (24%)
  between operations  0.65 us (2%)
    all_to_all x1, blocking collectives, body(): lax.all_to_all(stat, (CORE, 'grid'), split_axis=0, concat_axis=0, tiled=T...  16.4 us
    all_to_all x1, blocking collectives, body(): lax.all_to_all(packed, XY, split_axis=0, concat_axis=0, tiled=True)  14.5 us
    pallas_call x1, Pallas kernels, body(): pl.pallas_call(score_kernel, out_shape=(part, part, jax.ShapeDtypeStruct(...  7.97 us
    pallas_call x1, Pallas kernels, body(): pl.pallas_call(functools.partial(top_kernel, float(points ** 3)), out_sha...  1.42 us
  transfers between devices with their start and end apart: 1, of which 0 were waited for; matrix products, arithmetic and copies ran while one was open for 0% of the time, Pallas kernels for 0%

profile of v2, /device:TPU:2, one launch (start us, length us, event | category | flops | bytes accessed | tf_op | source)
XLA Modules:
  0.0 41.8 jit_solution(9161884927385727109)
XLA Ops:
  0.6 8.0 %scores.1 = (f32[32,8,16,128]{3,2,1,0:T(8,128)S(1)}, f32[32,8,16,128]{3,2,1,0:T(8,128)S(1)}, f32[16,8,128]{2,1,0:T(8,128)S(1)}) custom-call(f32[32,8,64,128]{3,2,1,0:T(8,128)} %x_hbm.1, bf16[256,256]{1,0:T(8,128)(2,1)} %constant.2.clone.w_hbm), custom_call_target="tpu_custom_call" | custom-call | tf_op jit(solution)/shard_map/scores/pallas_call | solution.py:212
  8.6 0.1 collective-permute-start
  8.7 16.4 %all_to_all.10.stat_ref = f32[16,8,128]{2,1,0:T(8,128)S(1)} all-to-all(f32[16,8,128]{2,1,0:T(8,128)S(1)} %get-tuple-element.7), channel_id=1, replica_groups=mesh['tmpl_0'=4,'tmpl_1'=4,'tmpl_2'=2,'grid'=8] {'tmpl_2','grid'}, dimensions={0} | all-to-all | bytes 131072 | tf_op jit(solution)/shard_map/all_to_all | solution.py:231
  25.1 0.0 collective-permute-done.other_ref
  25.1 1.4 %tops.1 = f32[640,128]{1,0:T(8,128)S(1)} custom-call(f32[32,8,16,128]{3,2,1,0:T(8,128)S(1)} %get-tuple-element.5.mine_ref, f32[32,8,16,128]{3,2,1,0:T(8,128)S(1)} %collective-permute-done.other_ref, f32[16,8,128]{2,1,0:T(8,128)S(1)} %all_to_all.10.stat_ref), custom_call_target="tpu_custom_call" | custom-call | tf_op jit(solution)/shard_map/tops/pallas_call | solution.py:233
  26.5 14.5 %all_to_all.11.in_ref = f32[16,5,8,128]{3,2,1,0:T(8,128)S(1)} all-to-all(f32[16,5,8,128]{3,2,1,0:T(8,128)S(1)} %bitcast.1), channel_id=1, replica_groups=mesh['tmpl_0'=4,'tmpl_1'=4,'tmpl_2'=2,'grid'=8] {'tmpl_0','tmpl_1'}, dimensions={0} | all-to-all | bytes 655360 | tf_op jit(solution)/shard_map/all_to_all | solution.py:246
  41.0 0.8 %finish.1 = (f32[4,8,2,64]{3,2,1,0:T(2,128)}, f32[8,2,64]{2,1,0:T(2,128)}) custom-call(f32[16,5,8,128]{3,2,1,0:T(8,128)S(1)} %all_to_all.11.in_ref), custom_call_target="tpu_custom_call" | custom-call | tf_op jit(solution)/shard_map/finish/pallas_call | solution.py:247
Async XLA Ops:
  8.6 16.5 %collective-permute-start = (f32[32,8,16,128]{3,2,1,0:T(8,128)S(1)}, f32[32,8,16,128]{3,2,1,0:T(8,128)S(1)}, u32[]{:S(2)}, u32[]{:S(2)}) collective-permute-start(f32[32,8,16,128]{3,2,1,0:T(8,128)S(1)} %get-tuple-element.6), channel_id=1, source_target_pairs={{0,8},{8,0},{1,9},{9,1},{2,10},{10,2},{3,11},{11,3},{4,12},{12,4},... | collective-permute-start | bytes 6291464 | tf_op jit(solution)/shard_map/ppermute | solution.py:232

commit v3 on v2

--- a/solution.py
+++ b/solution.py
@@ -14,7 +14,10 @@
 SPREAD_FLOOR = 0.25
 ROWS = 8
 LANES = 128
-GROUP = 4
+CHUNKS = (4,) * 8
+AHEAD = {0: 6, 1: 8}
+FIRST = 3
+LIVE = 4
 XY = ("tmpl_0", "tmpl_1")
 CORE = "tmpl_2"
 
@@ -56,14 +59,21 @@
     parities = (core, 1 - core)
     outs = (mine_ref, send_ref)
 
-    def fetch(g):
-        block = pl.ds(g * GROUP, GROUP)
-        return pltpu.make_async_copy(x_hbm.at[block], x_vmem.at[block], sems.at[g])
+    edges = [sum(CHUNKS[:c]) for c in range(len(CHUNKS) + 1)]
+    started = [0]
+
+    def fetch(c):
+        block = pl.ds(edges[c], CHUNKS[c])
+        return pltpu.make_async_copy(x_hbm.at[block], x_vmem.at[block], sems.at[c])
+
+    def fetch_up_to(c):
+        for ahead in range(started[0], c):
+            fetch(ahead).start()
+        started[0] = max(started[0], c)
 
     table = pltpu.make_async_copy(w_hbm, w_vmem, w_sem)
     table.start()
-    for g in range(tmpls // GROUP):
-        fetch(g).start()
+    fetch_up_to(FIRST)
     table.wait()
 
     def parts(t, parity):
@@ -99,23 +109,22 @@
             plain[t] = plain_t
             square[t] = square_t
 
-        def advance(g, carry):
-            fetch(g).wait()
-            for u in range(GROUP):
-                for m in range(2):
-                    for part in parts(g * GROUP + u, parities[m]):
-                        pltpu.matmul_acc_lhs(accs[2 * (u % 4) + m], part)
-                if u:
-                    take(g * GROUP + u - 1, (u - 1) % 4)
-            take(g * GROUP + GROUP - 1, (GROUP - 1) % 4)
-            return carry
-
-        lax.fori_loop(0, tmpls // GROUP, advance, 0)
+        for t in range(tmpls):
+            if t in edges:
+                c = edges.index(t)
+                fetch(c).wait()
+                fetch_up_to(AHEAD.get(c, 0))
+            for m in range(2):
+                for part in parts(t, parities[m]):
+                    pltpu.matmul_acc_lhs(accs[2 * (t % LIVE) + m], part)
+            if t:
+                take(t - 1, (t - 1) % LIVE)
+        take(tmpls - 1, (tmpls - 1) % LIVE)
 
     pl.run_scoped(
         run,
         *(pltpu.ACC(m)((16, 256), jnp.float32) for m in range(2)),
-        *(pltpu.ACC(m)((rows, 256), jnp.float32) for _ in range(4) for m in range(2)),
+        *(pltpu.ACC(m)((rows, 256), jnp.float32) for _ in range(LIVE) for m in range(2)),
     )
     totals = []
     for part in (plain, square):
@@ -219,7 +228,7 @@
             pltpu.VMEM((2 * doubled, 2 * doubled), jnp.bfloat16),
             pltpu.VMEM((tmpls, ROWS, LANES), jnp.float32),
             pltpu.VMEM((tmpls, ROWS, LANES), jnp.float32),
-            pltpu.SemaphoreType.DMA((tmpls // GROUP,)),
+            pltpu.SemaphoreType.DMA((len(CHUNKS),)),
             pltpu.SemaphoreType.DMA,
         ],
         compiler_params=pltpu.CompilerParams(vmem_limit_bytes=40 * 2**20),

time: 42.4 us -> 40.2 us (0.948)
  Pallas kernels: 10.1 us -> 7.87 us
    pallas_call x1, Pallas kernels: 7.97 us -> 5.7 us  [body(): pl.pallas_call(score_kernel, out_shape=(part, part, jax.ShapeDtypeStruct(...]
where the time goes in v3:
time: 40.2 us; the launch traced here: 39.5 us
  blocking collectives  30.9 us (77%)
  Pallas kernels  7.87 us (20%)
  between operations  0.65 us (2%)
    all_to_all x1, blocking collectives, body(): lax.all_to_all(stat, (CORE, 'grid'), split_axis=0, concat_axis=0, tiled=T...  16.4 us
    all_to_all x1, blocking collectives, body(): lax.all_to_all(packed, XY, split_axis=0, concat_axis=0, tiled=True)  14.5 us
    pallas_call x1, Pallas kernels, body(): pl.pallas_call(score_kernel, out_shape=(part, part, jax.ShapeDtypeStruct(...  5.7 us
    pallas_call x1, Pallas kernels, body(): pl.pallas_call(functools.partial(top_kernel, float(points ** 3)), out_sha...  1.42 us
  transfers between devices with their start and end apart: 1, of which 0 were waited for; matrix products, arithmetic and copies ran while one was open for 0% of the time, Pallas kernels for 0%

profile of v3, /device:TPU:2, one launch (start us, length us, event | category | flops | bytes accessed | tf_op | source)
XLA Modules:
  0.0 39.5 jit_solution(11037861278296935672)
XLA Ops:
  0.6 5.7 %scores.1 = (f32[32,8,16,128]{3,2,1,0:T(8,128)S(1)}, f32[32,8,16,128]{3,2,1,0:T(8,128)S(1)}, f32[16,8,128]{2,1,0:T(8,128)S(1)}) custom-call(f32[32,8,64,128]{3,2,1,0:T(8,128)} %x_hbm.1, bf16[256,256]{1,0:T(8,128)(2,1)} %constant.2.clone.w_hbm), custom_call_target="tpu_custom_call" | custom-call | tf_op jit(solution)/shard_map/scores/pallas_call | solution.py:221
  6.3 0.1 collective-permute-start
  6.4 16.4 %all_to_all.10.stat_ref = f32[16,8,128]{2,1,0:T(8,128)S(1)} all-to-all(f32[16,8,128]{2,1,0:T(8,128)S(1)} %get-tuple-element.7), channel_id=1, replica_groups=mesh['tmpl_0'=4,'tmpl_1'=4,'tmpl_2'=2,'grid'=8] {'tmpl_2','grid'}, dimensions={0} | all-to-all | bytes 131072 | tf_op jit(solution)/shard_map/all_to_all | solution.py:240
  22.8 0.0 collective-permute-done.other_ref
  22.8 1.4 %tops.1 = f32[640,128]{1,0:T(8,128)S(1)} custom-call(f32[32,8,16,128]{3,2,1,0:T(8,128)S(1)} %get-tuple-element.5.mine_ref, f32[32,8,16,128]{3,2,1,0:T(8,128)S(1)} %collective-permute-done.other_ref, f32[16,8,128]{2,1,0:T(8,128)S(1)} %all_to_all.10.stat_ref), custom_call_target="tpu_custom_call" | custom-call | tf_op jit(solution)/shard_map/tops/pallas_call | solution.py:242
  24.2 14.5 %all_to_all.11.in_ref = f32[16,5,8,128]{3,2,1,0:T(8,128)S(1)} all-to-all(f32[16,5,8,128]{3,2,1,0:T(8,128)S(1)} %bitcast.1), channel_id=1, replica_groups=mesh['tmpl_0'=4,'tmpl_1'=4,'tmpl_2'=2,'grid'=8] {'tmpl_0','tmpl_1'}, dimensions={0} | all-to-all | bytes 655360 | tf_op jit(solution)/shard_map/all_to_all | solution.py:255
  38.7 0.8 %finish.1 = (f32[4,8,2,64]{3,2,1,0:T(2,128)}, f32[8,2,64]{2,1,0:T(2,128)}) custom-call(f32[16,5,8,128]{3,2,1,0:T(8,128)S(1)} %all_to_all.11.in_ref), custom_call_target="tpu_custom_call" | custom-call | tf_op jit(solution)/shard_map/finish/pallas_call | solution.py:256
Async XLA Ops:
  6.3 16.5 %collective-permute-start = (f32[32,8,16,128]{3,2,1,0:T(8,128)S(1)}, f32[32,8,16,128]{3,2,1,0:T(8,128)S(1)}, u32[]{:S(2)}, u32[]{:S(2)}) collective-permute-start(f32[32,8,16,128]{3,2,1,0:T(8,128)S(1)} %get-tuple-element.6), channel_id=1, source_target_pairs={{0,8},{8,0},{1,9},{9,1},{2,10},{10,2},{3,11},{11,3},{4,12},{12,4},... | collective-permute-start | bytes 6291464 | tf_op jit(solution)/shard_map/ppermute | solution.py:241

commit v4 on v3

--- a/solution.py
+++ b/solution.py
@@ -18,6 +18,8 @@
 AHEAD = {0: 6, 1: 8}
 FIRST = 3
 LIVE = 4
+STAT_ORDER = [(c, z) for c in (1, 0) for z in (4, 5, 6, 7, 0, 1, 2, 3)]
+CHIP_ORDER = (10, 15, 14, 11, 9, 6, 13, 7, 12, 8, 5, 3, 2, 4, 1, 0)
 XY = ("tmpl_0", "tmpl_1")
 CORE = "tmpl_2"
 
@@ -157,11 +159,10 @@
     return a, b, c, d
 
 
-def top_kernel(count, mine_ref, other_ref, stat_ref, out_ref, gain_ref, shift_ref):
+def top_kernel(count, mine_ref, other_ref, stat_ref, out_ref, gain_ref, shift_ref, staged):
     tmpls, slab, pairs, _ = mine_ref.shape
-    peers = stat_ref.shape[0] // 2
     for half in range(2):
-        total = jnp.sum(stat_ref[half * peers : (half + 1) * peers], axis=0)
+        total = sum(stat_ref[p] for p, (c, _) in enumerate(STAT_ORDER) if c == half)
         average = total[0:1] / count
         spread = total[1:2] / count - average * average
         gain = 1.0 / jnp.sqrt(spread + SPREAD_FLOOR)
@@ -187,10 +188,13 @@
                     best = four if best is None else merge4(best, four)
             for r, value in enumerate((*best, total)):
                 start = (q * ROWS * (TOP + 1) + r) * slab + a
-                out_ref[pl.ds(start, ROWS, stride=(TOP + 1) * slab)] = value
+                staged[pl.ds(start, ROWS, stride=(TOP + 1) * slab)] = value
         return carry
 
     lax.fori_loop(0, slab, tile, 0)
+    size = (TOP + 1) * slab
+    for place, chip in enumerate(CHIP_ORDER):
+        out_ref[place * size : (place + 1) * size] = staged[chip * size : (chip + 1) * size]
 
 
 def final_kernel(norm, in_ref, best_ref, sum_ref):
@@ -237,7 +241,10 @@
         pltpu.with_memory_space_constraint(a, pltpu.HBM)
         for a in (spectrum, jnp.asarray(split_table(points)))
     ))
-    stats = lax.all_to_all(stat, (CORE, "grid"), split_axis=0, concat_axis=0, tiled=True)
+    meeting = [[c * lax.axis_size("grid") + z for c, z in STAT_ORDER]]
+    stats = lax.all_to_all(
+        stat, (CORE, "grid"), split_axis=0, concat_axis=0, axis_index_groups=meeting, tiled=True
+    )
     other = lax.ppermute(send, CORE, [(0, 1), (1, 0)])
     packed = pl.pallas_call(
         functools.partial(top_kernel, float(points**3)),
@@ -247,12 +254,15 @@
         scratch_shapes=[
             pltpu.VMEM((2 * tmpls, LANES), jnp.float32),
             pltpu.VMEM((2 * tmpls, LANES), jnp.float32),
+            pltpu.VMEM((chips * (TOP + 1) * slab, LANES), jnp.float32),
         ],
         compiler_params=pltpu.CompilerParams(vmem_limit_bytes=20 * 2**20),
         name="tops",
     )(mine, other, stats)
     packed = packed.reshape(chips, TOP + 1, slab, LANES)
-    received = lax.all_to_all(packed, XY, split_axis=0, concat_axis=0, tiled=True)
+    received = lax.all_to_all(
+        packed, XY, split_axis=0, concat_axis=0, axis_index_groups=[list(CHIP_ORDER)], tiled=True
+    )
     return pl.pallas_call(
         functools.partial(final_kernel, math.sqrt(2 * chips * tmpls)),
         out_shape=(

time: 40.2 us -> 35.4 us (0.88)
  blocking collectives: 30.9 us -> 26.3 us
    all_to_all x2, blocking collectives: 30.9 us -> 26.3 us  [the longest x1 13.2 us: body(): lax.all_to_all(stat, (CORE, 'grid'), split_axis=0, concat_axis=0, axis_in...]
where the time goes in v4:
time: 35.4 us; the launch traced here: 34.9 us
  blocking collectives  26.3 us (74%)
  Pallas kernels  7.89 us (22%)
  between operations  0.65 us (2%)
    all_to_all x1, blocking collectives, body(): lax.all_to_all(stat, (CORE, 'grid'), split_axis=0, concat_axis=0, axis_in...  13.2 us
    all_to_all x1, blocking collectives, body(): lax.all_to_all(packed, XY, split_axis=0, concat_axis=0, axis_index_groups...  13.2 us
    pallas_call x1, Pallas kernels, body(): pl.pallas_call(score_kernel, out_shape=(part, part, jax.ShapeDtypeStruct(...  5.7 us
    pallas_call x1, Pallas kernels, body(): pl.pallas_call(functools.partial(top_kernel, float(points ** 3)), out_sha...  1.44 us
    pallas_call x1, Pallas kernels, body(): pl.pallas_call(functools.partial(final_kernel, math.sqrt(2 * chips * tmpl...  0.75 us
  transfers between devices with their start and end apart: 1, of which 0 were waited for; matrix products, arithmetic and copies ran while one was open for 0% of the time, Pallas kernels for 0%

profile of v4, /device:TPU:2, one launch (start us, length us, event | category | flops | bytes accessed | tf_op | source)
XLA Modules:
  0.0 34.9 jit_solution(8152671771859573253)
XLA Ops:
  0.6 5.7 %scores.1 = (f32[32,8,16,128]{3,2,1,0:T(8,128)S(1)}, f32[32,8,16,128]{3,2,1,0:T(8,128)S(1)}, f32[16,8,128]{2,1,0:T(8,128)S(1)}) custom-call(f32[32,8,64,128]{3,2,1,0:T(8,128)} %x_hbm.1, bf16[256,256]{1,0:T(8,128)(2,1)} %constant.2.clone.w_hbm), custom_call_target="tpu_custom_call" | custom-call | tf_op jit(solution)/shard_map/scores/pallas_call | solution.py:225
  6.3 0.1 collective-permute-start
  6.4 13.2 %all_to_all.10.stat_ref = f32[16,8,128]{2,1,0:T(8,128)S(1)} all-to-all(f32[16,8,128]{2,1,0:T(8,128)S(1)} %get-tuple-element.7), channel_id=1, replica_groups={{12,13,14,15,8,9,10,11,4,5,6,7,0,1,2,3},{28,29,30,31,24,25,26,27,20,21,..., dimensions={0} | all-to-all | bytes 131072 | tf_op jit(solution)/shard_map/all_to_all | solution.py:245
  19.6 0.0 collective-permute-done.other_ref
  19.6 1.4 %tops.1 = f32[640,128]{1,0:T(8,128)S(1)} custom-call(f32[32,8,16,128]{3,2,1,0:T(8,128)S(1)} %get-tuple-element.5.mine_ref, f32[32,8,16,128]{3,2,1,0:T(8,128)S(1)} %collective-permute-done.other_ref, f32[16,8,128]{2,1,0:T(8,128)S(1)} %all_to_all.10.stat_ref), custom_call_target="tpu_custom_call" | custom-call | tf_op jit(solution)/shard_map/tops/pallas_call | solution.py:249
  21.0 13.2 %all_to_all.11.in_ref = f32[16,5,8,128]{3,2,1,0:T(8,128)S(1)} all-to-all(f32[16,5,8,128]{3,2,1,0:T(8,128)S(1)} %bitcast.1), channel_id=1, replica_groups={{160,240,224,176,144,96,208,112,192,128,80,48,32,64,16,0},{161,241,225,..., dimensions={0} | all-to-all | bytes 655360 | tf_op jit(solution)/shard_map/all_to_all | solution.py:263
  34.2 0.8 %finish.1 = (f32[4,8,2,64]{3,2,1,0:T(2,128)}, f32[8,2,64]{2,1,0:T(2,128)}) custom-call(f32[16,5,8,128]{3,2,1,0:T(8,128)S(1)} %all_to_all.11.in_ref), custom_call_target="tpu_custom_call" | custom-call | tf_op jit(solution)/shard_map/finish/pallas_call | solution.py:266
Async XLA Ops:
  6.3 13.3 %collective-permute-start = (f32[32,8,16,128]{3,2,1,0:T(8,128)S(1)}, f32[32,8,16,128]{3,2,1,0:T(8,128)S(1)}, u32[]{:S(2)}, u32[]{:S(2)}) collective-permute-start(f32[32,8,16,128]{3,2,1,0:T(8,128)S(1)} %get-tuple-element.6), channel_id=1, source_target_pairs={{0,8},{8,0},{1,9},{9,1},{2,10},{10,2},{3,11},{11,3},{4,12},{12,4},... | collective-permute-start | bytes 6291464 | tf_op jit(solution)/shard_map/ppermute | solution.py:248

commit v5 on v4

--- a/solution.py
+++ b/solution.py
@@ -37,17 +37,18 @@
     return np.concatenate(pair, axis=1).astype(jnp.bfloat16)
 
 
-def to_row(column):
-    count = column.shape[0]
+def diagonal(count, first):
     sub = lax.broadcasted_iota(jnp.int32, (count, LANES), 0)
     lane = lax.broadcasted_iota(jnp.int32, (count, LANES), 1)
-    return jnp.sum(jnp.where(sub == lane, column, 0.0), axis=0, keepdims=True)
-
-
-def to_column(row, count):
-    sub = lax.broadcasted_iota(jnp.int32, (count, LANES), 0)
-    lane = lax.broadcasted_iota(jnp.int32, (count, LANES), 1)
-    kept = jnp.sum(jnp.where(sub == lane, row, 0.0), axis=1, keepdims=True)
+    return lane == sub + first
+
+
+def to_row(column, first):
+    return jnp.sum(jnp.where(diagonal(column.shape[0], first), column, 0.0), axis=0, keepdims=True)
+
+
+def to_column(row, count, first):
+    kept = jnp.sum(jnp.where(diagonal(count, first), row, 0.0), axis=1, keepdims=True)
     return jnp.broadcast_to(kept, (count, LANES))
 
 
@@ -128,13 +129,11 @@
         *(pltpu.ACC(m)((16, 256), jnp.float32) for m in range(2)),
         *(pltpu.ACC(m)((rows, 256), jnp.float32) for _ in range(LIVE) for m in range(2)),
     )
-    totals = []
-    for part in (plain, square):
+    row = 0.0
+    for i, part in enumerate((plain, square)):
         whole = jnp.sum(part[...], axis=1)
-        totals.append(to_row(jnp.sum(whole, axis=1, keepdims=True)))
-    sub = lax.broadcasted_iota(jnp.int32, (ROWS, LANES), 0)
-    tile = jnp.where(sub == 0, totals[0], jnp.where(sub == 1, totals[1], 0.0))
-    stat_ref[...] = jnp.broadcast_to(tile[None], stat_ref.shape)
+        row = row + to_row(jnp.sum(whole, axis=1, keepdims=True), i * tmpls)
+    stat_ref[...] = jnp.broadcast_to(row[None], stat_ref.shape)
 
 
 def order(a, b):
@@ -163,11 +162,10 @@
     tmpls, slab, pairs, _ = mine_ref.shape
     for half in range(2):
         total = sum(stat_ref[p] for p, (c, _) in enumerate(STAT_ORDER) if c == half)
-        average = total[0:1] / count
-        spread = total[1:2] / count - average * average
-        gain = 1.0 / jnp.sqrt(spread + SPREAD_FLOOR)
-        gain_ref[pl.ds(half * tmpls, tmpls)] = to_column(gain, tmpls)
-        shift_ref[pl.ds(half * tmpls, tmpls)] = to_column(average, tmpls)
+        average = to_column(total, tmpls, 0) / count
+        spread = to_column(total, tmpls, tmpls) / count - average * average
+        gain_ref[pl.ds(half * tmpls, tmpls)] = 1.0 / jnp.sqrt(spread + SPREAD_FLOOR)
+        shift_ref[pl.ds(half * tmpls, tmpls)] = average
     core = lax.axis_index(CORE)
     firsts = (core * tmpls, (1 - core) * tmpls)
 
@@ -224,7 +222,7 @@
     part = jax.ShapeDtypeStruct((tmpls, slab, pairs, LANES), jnp.float32)
     mine, send, stat = pl.pallas_call(
         score_kernel,
-        out_shape=(part, part, jax.ShapeDtypeStruct((peers, ROWS, LANES), jnp.float32)),
+        out_shape=(part, part, jax.ShapeDtypeStruct((peers, 1, LANES), jnp.float32)),
         in_specs=[pl.BlockSpec(memory_space=pltpu.HBM)] * 2,
         out_specs=(vmem, vmem, vmem),
         scratch_shapes=[

time: 35.4 us -> 34.2 us (0.966)
  blocking collectives: 26.3 us -> 25.4 us
    all_to_all x1, blocking collectives: 13.2 us -> 12.4 us  [body(): lax.all_to_all(stat, (CORE, 'grid'), split_axis=0, concat_axis=0, axis_in...]
where the time goes in v5:
time: 34.2 us; the launch traced here: 34 us
  blocking collectives  25.4 us (74%)
  Pallas kernels  7.9 us (23%)
  between operations  0.65 us (2%)
    all_to_all x1, blocking collectives, body(): lax.all_to_all(packed, XY, split_axis=0, concat_axis=0, axis_index_groups...  13 us
    all_to_all x1, blocking collectives, body(): lax.all_to_all(stat, (CORE, 'grid'), split_axis=0, concat_axis=0, axis_in...  12.4 us
    pallas_call x1, Pallas kernels, body(): pl.pallas_call(score_kernel, out_shape=(part, part, jax.ShapeDtypeStruct(...  5.7 us
    pallas_call x1, Pallas kernels, body(): pl.pallas_call(functools.partial(top_kernel, float(points ** 3)), out_sha...  1.45 us
    pallas_call x1, Pallas kernels, body(): pl.pallas_call(functools.partial(final_kernel, math.sqrt(2 * chips * tmpl...  0.75 us
  transfers between devices with their start and end apart: 1, of which 0 were waited for; matrix products, arithmetic and copies ran while one was open for 0% of the time, Pallas kernels for 0%

profile of v5, /device:TPU:2, one launch (start us, length us, event | category | flops | bytes accessed | tf_op | source)
XLA Modules:
  0.0 34.0 jit_solution(6409847286394712469)
XLA Ops:
  0.6 5.7 %scores.1 = (f32[32,8,16,128]{3,2,1,0:T(8,128)S(1)}, f32[32,8,16,128]{3,2,1,0:T(8,128)S(1)}, f32[16,1,128]{2,1,0:T(1,128)S(1)}) custom-call(f32[32,8,64,128]{3,2,1,0:T(8,128)} %x_hbm.1, bf16[256,256]{1,0:T(8,128)(2,1)} %constant.2.clone.w_hbm), custom_call_target="tpu_custom_call" | custom-call | tf_op jit(solution)/shard_map/scores/pallas_call | solution.py:223
  6.3 0.1 collective-permute-start
  6.4 12.4 %all_to_all.10.stat_ref = f32[16,1,128]{2,1,0:T(1,128)S(1)} all-to-all(f32[16,1,128]{2,1,0:T(1,128)S(1)} %get-tuple-element.7), channel_id=1, replica_groups={{12,13,14,15,8,9,10,11,4,5,6,7,0,1,2,3},{28,29,30,31,24,25,26,27,20,21,..., dimensions={0} | all-to-all | bytes 16384 | tf_op jit(solution)/shard_map/all_to_all | solution.py:243
  18.8 0.0 collective-permute-done.other_ref
  18.8 1.5 %tops.1 = f32[640,128]{1,0:T(8,128)S(1)} custom-call(f32[32,8,16,128]{3,2,1,0:T(8,128)S(1)} %get-tuple-element.5.mine_ref, f32[32,8,16,128]{3,2,1,0:T(8,128)S(1)} %collective-permute-done.other_ref, f32[16,1,128]{2,1,0:T(1,128)S(1)} %all_to_all.10.stat_ref), custom_call_target="tpu_custom_call" | custom-call | tf_op jit(solution)/shard_map/tops/pallas_call | solution.py:247
  20.3 13.0 %all_to_all.11.in_ref = f32[16,5,8,128]{3,2,1,0:T(8,128)S(1)} all-to-all(f32[16,5,8,128]{3,2,1,0:T(8,128)S(1)} %bitcast.1), channel_id=1, replica_groups={{160,240,224,176,144,96,208,112,192,128,80,48,32,64,16,0},{161,241,225,..., dimensions={0} | all-to-all | bytes 655360 | tf_op jit(solution)/shard_map/all_to_all | solution.py:261
  33.3 0.8 %finish.1 = (f32[4,8,2,64]{3,2,1,0:T(2,128)}, f32[8,2,64]{2,1,0:T(2,128)}) custom-call(f32[16,5,8,128]{3,2,1,0:T(8,128)S(1)} %all_to_all.11.in_ref), custom_call_target="tpu_custom_call" | custom-call | tf_op jit(solution)/shard_map/finish/pallas_call | solution.py:264
Async XLA Ops:
  6.3 12.5 %collective-permute-start = (f32[32,8,16,128]{3,2,1,0:T(8,128)S(1)}, f32[32,8,16,128]{3,2,1,0:T(8,128)S(1)}, u32[]{:S(2)}, u32[]{:S(2)}) collective-permute-start(f32[32,8,16,128]{3,2,1,0:T(8,128)S(1)} %get-tuple-element.6), channel_id=1, source_target_pairs={{0,8},{8,0},{1,9},{9,1},{2,10},{10,2},{3,11},{11,3},{4,12},{12,4},... | collective-permute-start | bytes 6291464 | tf_op jit(solution)/shard_map/ppermute | solution.py:246

commit v6 on v5

--- a/solution.py
+++ b/solution.py
@@ -18,7 +18,8 @@
 AHEAD = {0: 6, 1: 8}
 FIRST = 3
 LIVE = 4
-STAT_ORDER = [(c, z) for c in (1, 0) for z in (4, 5, 6, 7, 0, 1, 2, 3)]
+CORE_ORDER = (1, 0)
+GRID_ORDER = (4, 5, 6, 7, 0, 1, 2, 3)
 CHIP_ORDER = (10, 15, 14, 11, 9, 6, 13, 7, 12, 8, 5, 3, 2, 4, 1, 0)
 XY = ("tmpl_0", "tmpl_1")
 CORE = "tmpl_2"
@@ -47,13 +48,13 @@
     return jnp.sum(jnp.where(diagonal(column.shape[0], first), column, 0.0), axis=0, keepdims=True)
 
 
-def to_column(row, count, first):
-    kept = jnp.sum(jnp.where(diagonal(count, first), row, 0.0), axis=1, keepdims=True)
+def to_column(row, count):
+    kept = jnp.sum(jnp.where(diagonal(count, 0), row, 0.0), axis=1, keepdims=True)
     return jnp.broadcast_to(kept, (count, LANES))
 
 
 def score_kernel(
-    x_hbm, w_hbm, mine_ref, send_ref, stat_ref, x_vmem, w_vmem, plain, square, sems, w_sem
+    x_hbm, w_hbm, mine_ref, send_ref, stat_ref, x_vmem, w_vmem, plain, square, bases, sems, w_sem
 ):
     tmpls, slab, beta, doubled = x_vmem.shape
     pairs = beta // 4
@@ -79,17 +80,22 @@
     fetch_up_to(FIRST)
     table.wait()
 
-    def parts(t, parity):
+    def base_of(t):
+        some = x_vmem[t, : slab // 4].reshape(-1, ROWS, LANES)
+        mean = jnp.sum(jnp.sum(some, axis=0), axis=0, keepdims=True) / (slab // 4 * beta)
+        lane = lax.broadcasted_iota(jnp.int32, (1, LANES), 1)
+        base = jnp.where(lane == 0, mean, 0.0)
+        bases[pl.ds(t, 1)] = base
+        return base
+
+    def parts(t, parity, base):
         sides = [
-            x_vmem[t, :, pl.ds(2 * parity + h, pairs, stride=4), :].reshape(rows, doubled)
+            x_vmem[t, :, pl.ds(2 * parity + h, pairs, stride=4), :].reshape(rows, doubled) - base
             for h in range(2)
         ]
         x = jnp.concatenate(sides, axis=1)
         high = x.astype(jnp.bfloat16)
-        rest = x - high.astype(jnp.float32)
-        mid = rest.astype(jnp.bfloat16)
-        low = (rest - mid.astype(jnp.float32)).astype(jnp.bfloat16)
-        return low, mid, high
+        return (x - high.astype(jnp.float32)).astype(jnp.bfloat16), high
 
     def run(*accs):
         first, accs = accs[:2], accs[2:]
@@ -117,8 +123,9 @@
                 c = edges.index(t)
                 fetch(c).wait()
                 fetch_up_to(AHEAD.get(c, 0))
+            base = base_of(t)
             for m in range(2):
-                for part in parts(t, parities[m]):
+                for part in parts(t, parities[m], base):
                     pltpu.matmul_acc_lhs(accs[2 * (t % LIVE) + m], part)
             if t:
                 take(t - 1, (t - 1) % LIVE)
@@ -130,9 +137,8 @@
         *(pltpu.ACC(m)((rows, 256), jnp.float32) for _ in range(LIVE) for m in range(2)),
     )
     row = 0.0
-    for i, part in enumerate((plain, square)):
-        whole = jnp.sum(part[...], axis=1)
-        row = row + to_row(jnp.sum(whole, axis=1, keepdims=True), i * tmpls)
+    for i, part in enumerate((jnp.sum(plain[...], axis=1), jnp.sum(square[...], axis=1), bases[...])):
+        row = row + to_row(jnp.sum(part, axis=1, keepdims=True), i * tmpls)
     stat_ref[...] = jnp.broadcast_to(row[None], stat_ref.shape)
 
 
@@ -160,12 +166,22 @@
 
 def top_kernel(count, mine_ref, other_ref, stat_ref, out_ref, gain_ref, shift_ref, staged):
     tmpls, slab, pairs, _ = mine_ref.shape
-    for half in range(2):
-        total = sum(stat_ref[p] for p, (c, _) in enumerate(STAT_ORDER) if c == half)
-        average = to_column(total, tmpls, 0) / count
-        spread = to_column(total, tmpls, tmpls) / count - average * average
-        gain_ref[pl.ds(half * tmpls, tmpls)] = 1.0 / jnp.sqrt(spread + SPREAD_FLOOR)
-        shift_ref[pl.ds(half * tmpls, tmpls)] = average
+    peers = stat_ref.shape[0]
+    slabs = peers // 2
+    rows = stat_ref[...].reshape(peers, LANES)
+    turned = [rows] + [pltpu.roll(rows, LANES - i * tmpls, 1) for i in (1, 2)]
+    sub = lax.broadcasted_iota(jnp.int32, (slabs, LANES), 0)
+    here = sum(jnp.where(lax.axis_index("grid") == z, i, 0) for i, z in enumerate(GRID_ORDER))
+    for place, half in enumerate(CORE_ORDER):
+        plain, square, base = (v[place * slabs : (place + 1) * slabs] for v in turned)
+        average = jnp.sum(plain / count + base / slabs, axis=0, keepdims=True)
+        off = average - base
+        spread = square - 2.0 * off * plain + (count / slabs) * (off * off)
+        spread = jnp.sum(spread, axis=0, keepdims=True) / count
+        gain = 1.0 / jnp.sqrt(spread + SPREAD_FLOOR)
+        shift = jnp.sum(jnp.where(sub == here, off, 0.0), axis=0, keepdims=True)
+        gain_ref[pl.ds(half * tmpls, tmpls)] = to_column(gain, tmpls)
+        shift_ref[pl.ds(half * tmpls, tmpls)] = to_column(shift, tmpls)
     core = lax.axis_index(CORE)
     firsts = (core * tmpls, (1 - core) * tmpls)
 
@@ -230,6 +246,7 @@
             pltpu.VMEM((2 * doubled, 2 * doubled), jnp.bfloat16),
             pltpu.VMEM((tmpls, ROWS, LANES), jnp.float32),
             pltpu.VMEM((tmpls, ROWS, LANES), jnp.float32),
+            pltpu.VMEM((tmpls, LANES), jnp.float32),
             pltpu.SemaphoreType.DMA((len(CHUNKS),)),
             pltpu.SemaphoreType.DMA,
         ],
@@ -239,7 +256,7 @@
         pltpu.with_memory_space_constraint(a, pltpu.HBM)
         for a in (spectrum, jnp.asarray(split_table(points)))
     ))
-    meeting = [[c * lax.axis_size("grid") + z for c, z in STAT_ORDER]]
+    meeting = [[c * lax.axis_size("grid") + z for c in CORE_ORDER for z in GRID_ORDER]]
     stats = lax.all_to_all(
         stat, (CORE, "grid"), split_axis=0, concat_axis=0, axis_index_groups=meeting, tiled=True
     )

time: 34.2 us -> 33.7 us (0.985)
  Pallas kernels: 7.9 us -> 7.36 us
    pallas_call x1, Pallas kernels: 5.7 us -> 5.08 us  [body(): pl.pallas_call(score_kernel, out_shape=(part, part, jax.ShapeDtypeStruct(...]
where the time goes in v6:
time: 33.7 us; the launch traced here: 33.5 us
  blocking collectives  25.4 us (75%)
  Pallas kernels  7.36 us (22%)
  between operations  0.65 us (2%)
    all_to_all x1, blocking collectives, body(): lax.all_to_all(packed, XY, split_axis=0, concat_axis=0, axis_index_groups...  13 us
    all_to_all x1, blocking collectives, body(): lax.all_to_all(stat, (CORE, 'grid'), split_axis=0, concat_axis=0, axis_in...  12.4 us
    pallas_call x1, Pallas kernels, body(): pl.pallas_call(score_kernel, out_shape=(part, part, jax.ShapeDtypeStruct(...  5.08 us
    pallas_call x1, Pallas kernels, body(): pl.pallas_call(functools.partial(top_kernel, float(points ** 3)), out_sha...  1.53 us
    pallas_call x1, Pallas kernels, body(): pl.pallas_call(functools.partial(final_kernel, math.sqrt(2 * chips * tmpl...  0.75 us
  transfers between devices with their start and end apart: 1, of which 0 were waited for; matrix products, arithmetic and copies ran while one was open for 0% of the time, Pallas kernels for 0%

profile of v6, /device:TPU:2, one launch (start us, length us, event | category | flops | bytes accessed | tf_op | source)
XLA Modules:
  0.0 33.5 jit_solution(1175227963970575629)
XLA Ops:
  0.6 5.1 %scores.1 = (f32[32,8,16,128]{3,2,1,0:T(8,128)S(1)}, f32[32,8,16,128]{3,2,1,0:T(8,128)S(1)}, f32[16,1,128]{2,1,0:T(1,128)S(1)}) custom-call(f32[32,8,64,128]{3,2,1,0:T(8,128)} %x_hbm.1, bf16[256,256]{1,0:T(8,128)(2,1)} %constant.2.clone.w_hbm), custom_call_target="tpu_custom_call" | custom-call | tf_op jit(solution)/shard_map/scores/pallas_call | solution.py:239
  5.7 0.1 collective-permute-start
  5.8 12.4 %all_to_all.10.stat_ref = f32[16,1,128]{2,1,0:T(1,128)S(1)} all-to-all(f32[16,1,128]{2,1,0:T(1,128)S(1)} %get-tuple-element.7), channel_id=1, replica_groups={{12,13,14,15,8,9,10,11,4,5,6,7,0,1,2,3},{28,29,30,31,24,25,26,27,20,21,..., dimensions={0} | all-to-all | bytes 16384 | tf_op jit(solution)/shard_map/all_to_all | solution.py:260
  18.2 0.0 collective-permute-done.other_ref
  18.2 1.5 %tops.1 = f32[640,128]{1,0:T(8,128)S(1)} custom-call(f32[32,8,16,128]{3,2,1,0:T(8,128)S(1)} %get-tuple-element.5.mine_ref, f32[32,8,16,128]{3,2,1,0:T(8,128)S(1)} %collective-permute-done.other_ref, f32[16,1,128]{2,1,0:T(1,128)S(1)} %all_to_all.10.stat_ref), custom_call_target="tpu_custom_call" | custom-call | tf_op jit(solution)/shard_map/tops/pallas_call | solution.py:264
  19.8 13.0 %all_to_all.11.in_ref = f32[16,5,8,128]{3,2,1,0:T(8,128)S(1)} all-to-all(f32[16,5,8,128]{3,2,1,0:T(8,128)S(1)} %bitcast.1), channel_id=1, replica_groups={{160,240,224,176,144,96,208,112,192,128,80,48,32,64,16,0},{161,241,225,..., dimensions={0} | all-to-all | bytes 655360 | tf_op jit(solution)/shard_map/all_to_all | solution.py:278
  32.8 0.8 %finish.1 = (f32[4,8,2,64]{3,2,1,0:T(2,128)}, f32[8,2,64]{2,1,0:T(2,128)}) custom-call(f32[16,5,8,128]{3,2,1,0:T(8,128)S(1)} %all_to_all.11.in_ref), custom_call_target="tpu_custom_call" | custom-call | tf_op jit(solution)/shard_map/finish/pallas_call | solution.py:281
Async XLA Ops:
  5.7 12.5 %collective-permute-start = (f32[32,8,16,128]{3,2,1,0:T(8,128)S(1)}, f32[32,8,16,128]{3,2,1,0:T(8,128)S(1)}, u32[]{:S(2)}, u32[]{:S(2)}) collective-permute-start(f32[32,8,16,128]{3,2,1,0:T(8,128)S(1)} %get-tuple-element.6), channel_id=1, source_target_pairs={{0,8},{8,0},{1,9},{9,1},{2,10},{10,2},{3,11},{11,3},{4,12},{12,4},... | collective-permute-start | bytes 6291464 | tf_op jit(solution)/shard_map/ppermute | solution.py:263

commit v7 on v5

--- a/solution.py
+++ b/solution.py
@@ -14,9 +14,9 @@
 SPREAD_FLOOR = 0.25
 ROWS = 8
 LANES = 128
-CHUNKS = (4,) * 8
-AHEAD = {0: 6, 1: 8}
-FIRST = 3
+CHUNKS = (2, 2, 4, 8, 8, 8)
+AHEAD = {0: 5, 1: 6}
+FIRST = 4
 LIVE = 4
 STAT_ORDER = [(c, z) for c in (1, 0) for z in (4, 5, 6, 7, 0, 1, 2, 3)]
 CHIP_ORDER = (10, 15, 14, 11, 9, 6, 13, 7, 12, 8, 5, 3, 2, 4, 1, 0)

time: 34.2 us -> 34.1 us (level)
  no operation moved by 1% of the time
where the time goes in v7:
time: 34.1 us; the launch traced here: 33.9 us
  blocking collectives  25.4 us (74%)
  Pallas kernels  7.77 us (23%)
  between operations  0.65 us (2%)
    all_to_all x1, blocking collectives, body(): lax.all_to_all(packed, XY, split_axis=0, concat_axis=0, axis_index_groups...  13 us
    all_to_all x1, blocking collectives, body(): lax.all_to_all(stat, (CORE, 'grid'), split_axis=0, concat_axis=0, axis_in...  12.4 us
    pallas_call x1, Pallas kernels, body(): pl.pallas_call(score_kernel, out_shape=(part, part, jax.ShapeDtypeStruct(...  5.57 us
    pallas_call x1, Pallas kernels, body(): pl.pallas_call(functools.partial(top_kernel, float(points ** 3)), out_sha...  1.45 us
    pallas_call x1, Pallas kernels, body(): pl.pallas_call(functools.partial(final_kernel, math.sqrt(2 * chips * tmpl...  0.75 us
  transfers between devices with their start and end apart: 1, of which 0 were waited for; matrix products, arithmetic and copies ran while one was open for 0% of the time, Pallas kernels for 0%

profile of v7, /device:TPU:2, one launch (start us, length us, event | category | flops | bytes accessed | tf_op | source)
XLA Modules:
  0.0 33.9 jit_solution(2798328182735790127)
XLA Ops:
  0.6 5.6 %scores.1 = (f32[32,8,16,128]{3,2,1,0:T(8,128)S(1)}, f32[32,8,16,128]{3,2,1,0:T(8,128)S(1)}, f32[16,1,128]{2,1,0:T(1,128)S(1)}) custom-call(f32[32,8,64,128]{3,2,1,0:T(8,128)} %x_hbm.1, bf16[256,256]{1,0:T(8,128)(2,1)} %constant.2.clone.w_hbm), custom_call_target="tpu_custom_call" | custom-call | tf_op jit(solution)/shard_map/scores/pallas_call | solution.py:223
  6.2 0.1 collective-permute-start
  6.3 12.4 %all_to_all.10.stat_ref = f32[16,1,128]{2,1,0:T(1,128)S(1)} all-to-all(f32[16,1,128]{2,1,0:T(1,128)S(1)} %get-tuple-element.7), channel_id=1, replica_groups={{12,13,14,15,8,9,10,11,4,5,6,7,0,1,2,3},{28,29,30,31,24,25,26,27,20,21,..., dimensions={0} | all-to-all | bytes 16384 | tf_op jit(solution)/shard_map/all_to_all | solution.py:243
  18.7 0.0 collective-permute-done.other_ref
  18.7 1.5 %tops.1 = f32[640,128]{1,0:T(8,128)S(1)} custom-call(f32[32,8,16,128]{3,2,1,0:T(8,128)S(1)} %get-tuple-element.5.mine_ref, f32[32,8,16,128]{3,2,1,0:T(8,128)S(1)} %collective-permute-done.other_ref, f32[16,1,128]{2,1,0:T(1,128)S(1)} %all_to_all.10.stat_ref), custom_call_target="tpu_custom_call" | custom-call | tf_op jit(solution)/shard_map/tops/pallas_call | solution.py:247
  20.2 13.0 %all_to_all.11.in_ref = f32[16,5,8,128]{3,2,1,0:T(8,128)S(1)} all-to-all(f32[16,5,8,128]{3,2,1,0:T(8,128)S(1)} %bitcast.1), channel_id=1, replica_groups={{160,240,224,176,144,96,208,112,192,128,80,48,32,64,16,0},{161,241,225,..., dimensions={0} | all-to-all | bytes 655360 | tf_op jit(solution)/shard_map/all_to_all | solution.py:261
  33.2 0.8 %finish.1 = (f32[4,8,2,64]{3,2,1,0:T(2,128)}, f32[8,2,64]{2,1,0:T(2,128)}) custom-call(f32[16,5,8,128]{3,2,1,0:T(8,128)S(1)} %all_to_all.11.in_ref), custom_call_target="tpu_custom_call" | custom-call | tf_op jit(solution)/shard_map/finish/pallas_call | solution.py:264
Async XLA Ops:
  6.2 12.5 %collective-permute-start = (f32[32,8,16,128]{3,2,1,0:T(8,128)S(1)}, f32[32,8,16,128]{3,2,1,0:T(8,128)S(1)}, u32[]{:S(2)}, u32[]{:S(2)}) collective-permute-start(f32[32,8,16,128]{3,2,1,0:T(8,128)S(1)} %get-tuple-element.6), channel_id=1, source_target_pairs={{0,8},{8,0},{1,9},{9,1},{2,10},{10,2},{3,11},{11,3},{4,12},{12,4},... | collective-permute-start | bytes 6291464 | tf_op jit(solution)/shard_map/ppermute | solution.py:246

commit v8 on v7

--- a/solution.py
+++ b/solution.py
@@ -189,7 +189,7 @@
                 staged[pl.ds(start, ROWS, stride=(TOP + 1) * slab)] = value
         return carry
 
-    lax.fori_loop(0, slab, tile, 0)
+    lax.fori_loop(0, slab, tile, 0, unroll=4)
     size = (TOP + 1) * slab
     for place, chip in enumerate(CHIP_ORDER):
         out_ref[place * size : (place + 1) * size] = staged[chip * size : (chip + 1) * size]

time: 34.1 us -> 34 us (level)
  no operation moved by 1% of the time
where the time goes in v8:
time: 34 us; the launch traced here: 33.8 us
  blocking collectives  25.4 us (75%)
  Pallas kernels  7.64 us (22%)
  between operations  0.65 us (2%)
    all_to_all x1, blocking collectives, body(): lax.all_to_all(packed, XY, split_axis=0, concat_axis=0, axis_index_groups...  13 us
    all_to_all x1, blocking collectives, body(): lax.all_to_all(stat, (CORE, 'grid'), split_axis=0, concat_axis=0, axis_in...  12.4 us
    pallas_call x1, Pallas kernels, body(): pl.pallas_call(score_kernel, out_shape=(part, part, jax.ShapeDtypeStruct(...  5.57 us
    pallas_call x1, Pallas kernels, body(): pl.pallas_call(functools.partial(top_kernel, float(points ** 3)), out_sha...  1.32 us
    pallas_call x1, Pallas kernels, body(): pl.pallas_call(functools.partial(final_kernel, math.sqrt(2 * chips * tmpl...  0.75 us
  transfers between devices with their start and end apart: 1, of which 0 were waited for; matrix products, arithmetic and copies ran while one was open for 0% of the time, Pallas kernels for 0%

profile of v8, /device:TPU:2, one launch (start us, length us, event | category | flops | bytes accessed | tf_op | source)
XLA Modules:
  0.0 33.8 jit_solution(12545450501892009948)
XLA Ops:
  0.6 5.6 %scores.1 = (f32[32,8,16,128]{3,2,1,0:T(8,128)S(1)}, f32[32,8,16,128]{3,2,1,0:T(8,128)S(1)}, f32[16,1,128]{2,1,0:T(1,128)S(1)}) custom-call(f32[32,8,64,128]{3,2,1,0:T(8,128)} %x_hbm.1, bf16[256,256]{1,0:T(8,128)(2,1)} %constant.2.clone.w_hbm), custom_call_target="tpu_custom_call" | custom-call | tf_op jit(solution)/shard_map/scores/pallas_call | solution.py:223
  6.2 0.1 collective-permute-start
  6.3 12.4 %all_to_all.10.stat_ref = f32[16,1,128]{2,1,0:T(1,128)S(1)} all-to-all(f32[16,1,128]{2,1,0:T(1,128)S(1)} %get-tuple-element.7), channel_id=1, replica_groups={{12,13,14,15,8,9,10,11,4,5,6,7,0,1,2,3},{28,29,30,31,24,25,26,27,20,21,..., dimensions={0} | all-to-all | bytes 16384 | tf_op jit(solution)/shard_map/all_to_all | solution.py:243
  18.7 0.0 collective-permute-done.other_ref
  18.7 1.3 %tops.1 = f32[640,128]{1,0:T(8,128)S(1)} custom-call(f32[32,8,16,128]{3,2,1,0:T(8,128)S(1)} %get-tuple-element.5.mine_ref, f32[32,8,16,128]{3,2,1,0:T(8,128)S(1)} %collective-permute-done.other_ref, f32[16,1,128]{2,1,0:T(1,128)S(1)} %all_to_all.10.stat_ref), custom_call_target="tpu_custom_call" | custom-call | tf_op jit(solution)/shard_map/tops/pallas_call | solution.py:247
  20.0 13.0 %all_to_all.11.in_ref = f32[16,5,8,128]{3,2,1,0:T(8,128)S(1)} all-to-all(f32[16,5,8,128]{3,2,1,0:T(8,128)S(1)} %bitcast.1), channel_id=1, replica_groups={{160,240,224,176,144,96,208,112,192,128,80,48,32,64,16,0},{161,241,225,..., dimensions={0} | all-to-all | bytes 655360 | tf_op jit(solution)/shard_map/all_to_all | solution.py:261
  33.0 0.8 %finish.1 = (f32[4,8,2,64]{3,2,1,0:T(2,128)}, f32[8,2,64]{2,1,0:T(2,128)}) custom-call(f32[16,5,8,128]{3,2,1,0:T(8,128)S(1)} %all_to_all.11.in_ref), custom_call_target="tpu_custom_call" | custom-call | tf_op jit(solution)/shard_map/finish/pallas_call | solution.py:264
Async XLA Ops:
  6.2 12.5 %collective-permute-start = (f32[32,8,16,128]{3,2,1,0:T(8,128)S(1)}, f32[32,8,16,128]{3,2,1,0:T(8,128)S(1)}, u32[]{:S(2)}, u32[]{:S(2)}) collective-permute-start(f32[32,8,16,128]{3,2,1,0:T(8,128)S(1)} %get-tuple-element.6), channel_id=1, source_target_pairs={{0,8},{8,0},{1,9},{9,1},{2,10},{10,2},{3,11},{11,3},{4,12},{12,4},... | collective-permute-start | bytes 6291464 | tf_op jit(solution)/shard_map/ppermute | solution.py:246

commit v9 on v8

--- a/solution.py
+++ b/solution.py
@@ -55,7 +55,8 @@
 def score_kernel(
     x_hbm, w_hbm, mine_ref, send_ref, stat_ref, x_vmem, w_vmem, plain, square, sems, w_sem
 ):
-    tmpls, slab, beta, doubled = x_vmem.shape
+    _, slab, beta, doubled = x_vmem.shape
+    tmpls = mine_ref.shape[0]
     pairs = beta // 4
     rows = slab * pairs
     core = lax.axis_index(CORE)
@@ -226,7 +227,7 @@
         in_specs=[pl.BlockSpec(memory_space=pltpu.HBM)] * 2,
         out_specs=(vmem, vmem, vmem),
         scratch_shapes=[
-            pltpu.VMEM(spectrum.shape, jnp.float32),
+            pltpu.VMEM((tmpls + 1, *spectrum.shape[1:]), jnp.float32),
             pltpu.VMEM((2 * doubled, 2 * doubled), jnp.bfloat16),
             pltpu.VMEM((tmpls, ROWS, LANES), jnp.float32),
             pltpu.VMEM((tmpls, ROWS, LANES), jnp.float32),
@@ -250,9 +251,9 @@
         in_specs=[vmem, vmem, vmem],
         out_specs=vmem,
         scratch_shapes=[
-            pltpu.VMEM((2 * tmpls, LANES), jnp.float32),
-            pltpu.VMEM((2 * tmpls, LANES), jnp.float32),
-            pltpu.VMEM((chips * (TOP + 1) * slab, LANES), jnp.float32),
+            pltpu.VMEM((2 * tmpls + ROWS, LANES), jnp.float32),
+            pltpu.VMEM((2 * tmpls + ROWS, LANES), jnp.float32),
+            pltpu.VMEM(((chips + 1) * (TOP + 1) * slab, LANES), jnp.float32),
         ],
         compiler_params=pltpu.CompilerParams(vmem_limit_bytes=20 * 2**20),
         name="tops",

time: 34 us -> 34 us (level)
  no operation moved by 1% of the time
where the time goes in v9:
time: 34 us; the launch traced here: 33.9 us
  blocking collectives  25.4 us (75%)
  Pallas kernels  7.73 us (23%)
  between operations  0.65 us (2%)
    all_to_all x1, blocking collectives, body(): lax.all_to_all(packed, XY, split_axis=0, concat_axis=0, axis_index_groups...  13 us
    all_to_all x1, blocking collectives, body(): lax.all_to_all(stat, (CORE, 'grid'), split_axis=0, concat_axis=0, axis_in...  12.4 us
    pallas_call x1, Pallas kernels, body(): pl.pallas_call(score_kernel, out_shape=(part, part, jax.ShapeDtypeStruct(...  5.57 us
    pallas_call x1, Pallas kernels, body(): pl.pallas_call(functools.partial(top_kernel, float(points ** 3)), out_sha...  1.42 us
    pallas_call x1, Pallas kernels, body(): pl.pallas_call(functools.partial(final_kernel, math.sqrt(2 * chips * tmpl...  0.75 us
  transfers between devices with their start and end apart: 1, of which 0 were waited for; matrix products, arithmetic and copies ran while one was open for 0% of the time, Pallas kernels for 0%

profile of v9, /device:TPU:2, one launch (start us, length us, event | category | flops | bytes accessed | tf_op | source)
XLA Modules:
  0.0 33.9 jit_solution(4376828213983027895)
XLA Ops:
  0.6 5.6 %scores.1 = (f32[32,8,16,128]{3,2,1,0:T(8,128)S(1)}, f32[32,8,16,128]{3,2,1,0:T(8,128)S(1)}, f32[16,1,128]{2,1,0:T(1,128)S(1)}) custom-call(f32[32,8,64,128]{3,2,1,0:T(8,128)} %x_hbm.1, bf16[256,256]{1,0:T(8,128)(2,1)} %constant.2.clone.w_hbm), custom_call_target="tpu_custom_call" | custom-call | tf_op jit(solution)/shard_map/scores/pallas_call | solution.py:224
  6.2 0.1 collective-permute-start
  6.3 12.4 %all_to_all.10.stat_ref = f32[16,1,128]{2,1,0:T(1,128)S(1)} all-to-all(f32[16,1,128]{2,1,0:T(1,128)S(1)} %get-tuple-element.7), channel_id=1, replica_groups={{12,13,14,15,8,9,10,11,4,5,6,7,0,1,2,3},{28,29,30,31,24,25,26,27,20,21,..., dimensions={0} | all-to-all | bytes 16384 | tf_op jit(solution)/shard_map/all_to_all | solution.py:244
  18.7 0.0 collective-permute-done.other_ref
  18.7 1.4 %tops.1 = f32[640,128]{1,0:T(8,128)S(1)} custom-call(f32[32,8,16,128]{3,2,1,0:T(8,128)S(1)} %get-tuple-element.5.mine_ref, f32[32,8,16,128]{3,2,1,0:T(8,128)S(1)} %collective-permute-done.other_ref, f32[16,1,128]{2,1,0:T(1,128)S(1)} %all_to_all.10.stat_ref), custom_call_target="tpu_custom_call" | custom-call | tf_op jit(solution)/shard_map/tops/pallas_call | solution.py:248
  20.1 13.0 %all_to_all.11.in_ref = f32[16,5,8,128]{3,2,1,0:T(8,128)S(1)} all-to-all(f32[16,5,8,128]{3,2,1,0:T(8,128)S(1)} %bitcast.1), channel_id=1, replica_groups={{160,240,224,176,144,96,208,112,192,128,80,48,32,64,16,0},{161,241,225,..., dimensions={0} | all-to-all | bytes 655360 | tf_op jit(solution)/shard_map/all_to_all | solution.py:262
  33.1 0.8 %finish.1 = (f32[4,8,2,64]{3,2,1,0:T(2,128)}, f32[8,2,64]{2,1,0:T(2,128)}) custom-call(f32[16,5,8,128]{3,2,1,0:T(8,128)S(1)} %all_to_all.11.in_ref), custom_call_target="tpu_custom_call" | custom-call | tf_op jit(solution)/shard_map/finish/pallas_call | solution.py:265
Async XLA Ops:
  6.2 12.5 %collective-permute-start = (f32[32,8,16,128]{3,2,1,0:T(8,128)S(1)}, f32[32,8,16,128]{3,2,1,0:T(8,128)S(1)}, u32[]{:S(2)}, u32[]{:S(2)}) collective-permute-start(f32[32,8,16,128]{3,2,1,0:T(8,128)S(1)} %get-tuple-element.6), channel_id=1, source_target_pairs={{0,8},{8,0},{1,9},{9,1},{2,10},{10,2},{3,11},{11,3},{4,12},{12,4},... | collective-permute-start | bytes 6291464 | tf_op jit(solution)/shard_map/ppermute | solution.py:247
